TPU v7x, 64 devices: a 2x2x8 block of a 4x4x8 slice. The times are simulated.
64 devices in a mesh: dp: 4 (over x, y), ep: 16 (over z, core).
Axes of the slice: x: 2, y: 2, z: 8, core: 2. Of those that a mesh axis runs over, the one named last changes fastest.
The devices are a block of a 4x4x8 slice.
Arguments:
- tokens: bfloat16 [2048, 2048], P(('dp', 'ep')), parts along dimension 0
- expert_ids: int32 [2048, 8], P(('dp', 'ep')), parts along dimension 0
- gate_weights: float32 [2048, 8], P(('dp', 'ep')), parts along dimension 0
- slot_ids: int32 [2048, 8], P(('dp', 'ep')), parts along dimension 0
- w_gate: bfloat16 [64, 2048, 1024], P('ep')
- w_up: bfloat16 [64, 2048, 1024], P('ep')
- w_down: bfloat16 [64, 1024, 2048], P('ep')
Outputs:
- output: bfloat16 [2048, 2048], P(('dp', 'ep')), parts along dimension 0
There are 4 independent parts. A program takes and returns all parts, laid end to end along the dimension named above; an argument that names none is the same for every part.
All inputs are finite; a program needn't handle non-finite values.
Results may differ from a plain program's by a relative error of at most 0.00122.
Values are sent between devices in bfloat16 or wider.
A program may use at most 768 MiB of HBM per device.

v0:
```python
import jax
import jax.numpy as jnp
from jax import lax
from jax.sharding import PartitionSpec as P


def solution(mesh):
    row_spec = P(('dp', 'ep'), None)
    exp_spec = P('ep', None, None)

    def local_moe(tok_rows, expert_ids, gate_weights, slot_ids, w_gate, w_up, w_down):
        tok_loc, model_dim = tok_rows.shape
        top_k = expert_ids.shape[1]
        local_exp = w_gate.shape[0]
        capacity = 2 * top_k * tok_loc // local_exp
        num_rows = local_exp * capacity
        all_tok = lax.all_gather(tok_rows, 'ep', tiled=True)
        all_ids = lax.all_gather(expert_ids, 'ep', tiled=True)
        all_gates = lax.all_gather(gate_weights, 'ep', tiled=True)
        all_slots = lax.all_gather(slot_ids, 'ep', tiled=True)
        group_rows = all_tok.shape[0]
        local_ids = all_ids - lax.axis_index('ep') * local_exp
        is_owned = (local_ids >= 0) & (local_ids < local_exp)
        flat_ids = jnp.where(is_owned, local_ids * capacity + all_slots, num_rows).reshape(-1)
        tok_index = jnp.repeat(jnp.arange(group_rows, dtype=jnp.int32), top_k)
        src_rows = jnp.full((num_rows,), group_rows, jnp.int32).at[flat_ids].set(tok_index, mode='drop')
        gate_rows = jnp.zeros((num_rows,), jnp.float32).at[flat_ids].set(all_gates.reshape(-1), mode='drop')
        buffers = jnp.take(all_tok, src_rows, axis=0, mode='fill', fill_value=0).reshape(local_exp, capacity, model_dim)
        gate_h = jnp.einsum('ecd,edf->ecf', buffers, w_gate, preferred_element_type=jnp.float32)
        up_h = jnp.einsum('ecd,edf->ecf', buffers, w_up, preferred_element_type=jnp.float32)
        hidden = (jax.nn.silu(gate_h) * up_h).astype(jnp.bfloat16)
        exp_out = jnp.einsum('ecf,efd->ecd', hidden, w_down, preferred_element_type=jnp.float32)
        weighted = exp_out.reshape(num_rows, model_dim) * gate_rows[:, None]
        partial = jnp.zeros((group_rows, model_dim), jnp.float32).at[src_rows].add(weighted, mode='drop')
        summed = lax.psum_scatter(partial, 'ep', scatter_dimension=0, tiled=True)
        return summed.astype(jnp.bfloat16)

    return jax.shard_map(local_moe, mesh=mesh, in_specs=(row_spec, row_spec, row_spec, row_spec, exp_spec, exp_spec, exp_spec), out_specs=row_spec, check_vma=False)
```

profile of v0, /device:TPU:21, one launch (start us, length us, event | category | flops | bytes accessed | tf_op | source)
XLA Modules:
  0.0 205.4 jit_solution(5002800928050926779)
XLA Ops:
  6.5 0.0 all-gather.5.cloned.1.call-start
  6.6 0.7 all-gather.5.cloned.1.call-update
  7.3 0.1 reduce-scatter.2.cloned.1.call-start
  7.4 22.9 %all-gather = s32[16,32,8]{1,2,0:T(8,128)S(1)} all-gather(s32[1,32,8]{1,2,0:T(8,128)} %bitcast.18), channel_id=1, replica_groups=mesh['dp'=4,'ep'=16] {'ep'}, dimensions={0}, use_global_device_ids=true | all-gather | bytes 17408 | tf_op jit(solution)/shard_map/all_gather | solution.py:18
  30.3 14.9 %all-gather.1 = s32[16,32,8]{1,2,0:T(8,128)S(1)} all-gather(s32[1,32,8]{1,2,0:T(8,128)} %bitcast.19), channel_id=1, replica_groups=mesh['dp'=4,'ep'=16] {'ep'}, dimensions={0}, use_global_device_ids=true | all-gather | bytes 17408 | tf_op jit(solution)/shard_map/all_gather | solution.py:20
  45.3 0.1 copy.10
  45.4 0.2 reshape.53
  45.6 15.9 %all-gather.2 = f32[16,32,8]{1,2,0:T(8,128)S(1)} all-gather(f32[1,32,8]{1,2,0:T(8,128)} %bitcast.20), channel_id=1, replica_groups=mesh['dp'=4,'ep'=16] {'ep'}, dimensions={0}, use_global_device_ids=true | all-gather | bytes 17408 | tf_op jit(solution)/shard_map/all_gather | solution.py:19
  61.5 0.1 copy.11
  61.6 0.2 reshape.77
  61.8 0.1 reshape.69
  62.0 15.5 %scatter_custom_fusion.1 = f32[512]{0:T(512)S(1)} fusion(s32[4096]{0:T(1024)S(1)} %bitcast.16, f32[4096]{0:T(1024)S(1)} %reshape.77, f32[]{:T(128)} %constant.9.clone.1), kind=kCustom, calls=%fused_computation.20 | custom fusion | bytes 2052 | tf_op jit(solution)/shard_map/scatter | solution.py:27
  77.5 15.7 %scatter_custom_fusion = s32[512]{0:T(512)S(1)} fusion(s32[4096]{0:T(1024)S(1)} %bitcast.17, s32[4096]{0:T(1024)S(1)} %reshape.69, s32[]{:T(128)} %constant.10.clone.1), kind=kCustom, calls=%fused_computation.22 | custom fusion | bytes 2052 | tf_op jit(solution)/shard_map/scatter | solution.py:26
  93.2 0.0 all-gather.5.cloned.1.call-done
  93.3 6.3 %gather_fusion = bf16[512,2048]{1,0:T(8,128)(2,1)S(1)} fusion(bf16[512,2048]{1,0:T(8,128)(2,1)} %all-gather.5.cloned.1.call-done, s32[1024]{0:T(1024)S(1)} %pad_clamp_fusion), kind=kCustom, calls=%fused_computation | custom fusion | bytes 4196352 | tf_op jit(solution)/shard_map/jit(_take)/gather | solution.py:28
  99.5 9.5 %fusion.2 = f32[4,128,1024]{2,1,0:T(8,128)} fusion(bf16[4,2048,1024]{2,1,0:T(8,128)(2,1)} %param.12, bf16[4,128,2048]{2,1,0:T(8,128)(2,1)S(1)} %bitcast.14, pred[4,128]{1,0:T(4,128)(4,1)S(1)} %and_bitcast_fusion), kind=kOutput, calls=%fused_computation.9 | convolution fusion | flops 2148532224 | bytes 20972032 | tf_op jit(solution)/shard_map/ecd,edf->ecf/dot_general | solution.py:30
  109.0 17.9 %fusion.4 = f32[4,128,2048]{2,1,0:T(8,128)} fusion(bf16[4,1024,2048]{2,1,0:T(8,128)(2,1)} %param.13, f32[4,128,1024]{2,1,0:T(8,128)} %fusion.2, bf16[4,2048,1024]{2,1,0:T(8,128)(2,1)} %param.11, bf16[4,128,2048]{2,1,0:T(8,128)(2,1)S(1)} %bitcast.15, pred[4,128]{1,0:T(4,128)(4,1)S(1)} %and_bitcast_fusion), kind=kOutput, calls=%fused_computation.11 | convolution fusion | flops 4299161600 | bytes 41943552 | tf_op jit(solution)/shard_map/ecf,efd->ecd/dot_general | solution.py:32
  126.9 4.5 %bitcast_multiply_fusion = f32[512,2048]{1,0:T(8,128)} fusion(f32[4,128,2048]{2,1,0:T(8,128)} %fusion.4, f32[512]{0:T(512)S(1)} %scatter_custom_fusion.1), kind=kLoop, calls=%fused_computation.4 | loop fusion | flops 1048576 | bytes 8390656 | tf_op jit(solution)/shard_map/mul | solution.py:33
  131.4 10.8 %scatter_custom_fusion.2 = f32[512,2048]{1,0:T(8,128)} fusion(s32[512]{0:T(512)S(1)} %compare_select_fusion.1, f32[512,2048]{1,0:T(8,128)} %bitcast_multiply_fusion, f32[]{:T(128)} %constant.9.clone.1), kind=kCustom, calls=%fused_computation.6 | custom fusion | flops 1048576 | bytes 4194816 | tf_op jit(solution)/shard_map/scatter-add | solution.py:34
  142.2 0.1 reduce-scatter.2.cloned.1.call-update
  142.3 54.6 %reduce-scatter.2.cloned.1.call-done = f32[32,2048]{1,0:T(8,128)} async-done(((f32[512,2048]{1,0:T(8,128)}), f32[32,2048]{1,0:T(8,128)}) %reduce-scatter.2.cloned.1.call-update) | async-done | bytes 262160 | tf_op jit(solution)/shard_map/reduce_scatter | solution.py:35
  196.9 1.6 convert_element_type.7
  (6 shorter events, 0.1 us)
Async XLA Ops:
  6.5 86.7 %all-gather.5.cloned.1.call-start = ((), (), s32[]{:S(2)}) async-start(), calls=%async_computation.1 | async-start | bytes 2228224 | tf_op jit(solution)/shard_map/all_gather | solution.py:17
  7.3 189.6 %reduce-scatter.2.cloned.1.call-start = ((), (), s32[]{:S(2)}) async-start(), calls=%async_computation.2 | async-start | bytes 4456448 | tf_op jit(solution)/shard_map/reduce_scatter | solution.py:35
Sparse Core Ops, SparseCore 0:
  9.0 41.2 all-gather.4
  142.4 54.4 reduce-scatter.1
where the time goes:
time: 208 us; the launch traced here: 205 us
  waiting for transfers between devices  55.4 us (27%)
  blocking collectives  53.8 us (26%)
  local copies, waits for them, and re-layouts  38.2 us (18%)
  matrix products  27.4 us (13%)
  other arithmetic  17 us (8%)
  between operations  13.5 us (6%)
    reduce_scatter x1, waiting for transfers between devices, local_moe(): summed = lax.psum_scatter(partial, 'ep', scatter_dimension=0, tiled=True)  54.6 us
    all_gather x1, blocking collectives, local_moe(): all_ids = lax.all_gather(expert_ids, 'ep', tiled=True)  22.9 us
    dot_general x1, matrix products, local_moe(): jnp.einsum('ecf,efd->ecd', hidden, w_down, preferred_element_type=jnp.flo...  17.9 us
    all_gather x1, blocking collectives, local_moe(): all_gates = lax.all_gather(gate_weights, 'ep', tiled=True)  15.9 us
    scatter x1, local copies, waits for them, and re-layouts, local_moe(): jnp.full((num_rows,), group_rows, jnp.int32).at[flat_ids]  15.7 us
    scatter x1, local copies, waits for them, and re-layouts, local_moe(): jnp.zeros((num_rows,), jnp.float32).at[flat_ids]  15.5 us
    all_gather x1, blocking collectives, local_moe(): all_slots = lax.all_gather(slot_ids, 'ep', tiled=True)  14.9 us
    scatter-add x1, other arithmetic, local_moe(): jnp.zeros((group_rows, model_dim), jnp.float32).at[src_rows]  10.8 us
  transfers between devices with their start and end apart: 2, of which 1 were waited for; matrix products, arithmetic and copies ran while one was open for 16% of the time, Pallas kernels for 0%

commit v1 on v0

v1 whole, which is shorter than its diff:
```python
import functools

import jax
import jax.numpy as jnp
from jax import lax
from jax.experimental import pallas as pl
from jax.experimental.pallas import tpu as pltpu
from jax.sharding import PartitionSpec as P

CORES = 2
PIECES = 4
COLS = 256
DOWN_SLOTS = 6
MESH = pl.DeviceIdType.MESH
F32 = jnp.float32
BF16 = jnp.bfloat16


def moe_kernel(nz, capacity, tok_hbm, ids_ref, slots_ref, gates_ref, wg_hbm, wu_hbm, wd_hbm, out_ref,
               tok_all, meta_all, wg, wu, wd, pick, pick_t, slot_gate, buf, hid, parts,
               acc, die_out, die_in, ring0, ring1, ring2, ring3,
               in_sem, gate_sem, down_sem, ag_send, ag_recv, agm_send, agm_recv, die_send, die_recv,
               diem_send, diem_recv, sum_send, sum_recv, rs_send, rs_recv):
    rows = tok_hbm.shape[0]
    dim = tok_hbm.shape[1]
    n_exp, _, ffn = wg.shape
    n_col = dim // COLS
    half = rows // 2
    far = nz // 2
    side = nz * rows
    me = lax.axis_index('ep')
    z = me // CORES
    core = me % CORES
    right = {'ep': ((z + 1) % nz) * CORES + core}
    left = {'ep': ((z + nz - 1) % nz) * CORES + core}
    partner = {'ep': z * CORES + (1 - core)}
    nbr = (right, left)
    piece = dim // PIECES

    own = pltpu.make_async_copy(tok_hbm, tok_all.at[0], in_sem)
    own.start()

    def gate_copies(e):
        return (pltpu.make_async_copy(wg_hbm.at[e], wg.at[e], gate_sem.at[e, 0]),
                pltpu.make_async_copy(wu_hbm.at[e], wu.at[e], gate_sem.at[e, 1]))

    def down_copy(q):
        cols = pl.ds(pl.multiple_of(q * COLS, COLS), COLS)
        return pltpu.make_async_copy(wd_hbm.at[:, :, cols], wd.at[lax.rem(q, DOWN_SLOTS)], down_sem.at[q])

    for e in range(n_exp):
        for copy in gate_copies(e):
            copy.start(priority=1)
    for q in range(min(DOWN_SLOTS, n_col)):
        down_copy(q).start(priority=1)

    barrier = pltpu.get_barrier_semaphore()
    for dev in (right, left, partner):
        pl.semaphore_signal(barrier, inc=1, device_id=dev, device_id_type=MESH)

    meta_all[0] = jnp.concatenate(
        [ids_ref[...].astype(F32), slots_ref[...].astype(F32), gates_ref[...],
         jnp.zeros(gates_ref.shape, F32)], axis=1)
    pl.semaphore_wait(barrier, 3)
    own.wait()

    def cols_of(p):
        return pl.ds(p * piece, piece)

    def ring_copy(way, hop, p):
        src = (nz - hop + 1) % nz if way == 0 else hop - 1
        dst = nz - hop if way == 0 else hop
        return pltpu.make_async_remote_copy(
            tok_all.at[src, :, cols_of(p)], tok_all.at[dst, :, cols_of(p)],
            ag_send.at[way, hop - 1, p], ag_recv.at[way, hop - 1, p], device_id=nbr[way], device_id_type=MESH)

    def ring_meta(way, hop):
        src = (nz - hop + 1) % nz if way == 0 else hop - 1
        dst = nz - hop if way == 0 else hop
        return pltpu.make_async_remote_copy(
            meta_all.at[src], meta_all.at[dst], agm_send.at[way, hop - 1], agm_recv.at[way, hop - 1],
            device_id=nbr[way], device_id_type=MESH)

    def die_copy(j, p):
        return pltpu.make_async_remote_copy(
            tok_all.at[j, :, cols_of(p)], tok_all.at[nz + j, :, cols_of(p)],
            die_send.at[j, p], die_recv.at[j, p], device_id=partner, device_id_type=MESH)

    def die_meta(j):
        return pltpu.make_async_remote_copy(
            meta_all.at[j], meta_all.at[nz + j], diem_send.at[j], diem_recv.at[j],
            device_id=partner, device_id_type=MESH)

    def on_ring(way, hop, p):
        if hop < far:
            return True
        return hop == far and (p < PIECES // 2) == (way == 0)

    def meta_on_ring(way, hop):
        return hop < far or (hop == far and way == 0)

    for way in range(2):
        ring_meta(way, 1).start()
    for p in range(PIECES):
        for way in range(2):
            if on_ring(way, 1, p):
                ring_copy(way, 1, p).start()
    die_meta(0).start()
    for p in range(PIECES):
        die_copy(0, p).start()

    def take_meta(hop):
        for way in range(2):
            if meta_on_ring(way, hop):
                ring_meta(way, hop).wait_recv()
                if meta_on_ring(way, hop + 1):
                    ring_meta(way, hop + 1).start()
                die_meta(nz - hop if way == 0 else hop).start()

    def take_tokens(hop):
        for p in range(PIECES):
            for way in range(2):
                if on_ring(way, hop, p):
                    ring_copy(way, hop, p).wait_recv()
                    if on_ring(way, hop + 1, p):
                        ring_copy(way, hop + 1, p).start()
                    die_copy(nz - hop if way == 0 else hop, p).start()

    for hop in range(1, far):
        take_meta(hop)
        take_tokens(hop)
    take_meta(far)
    for j in range(nz):
        die_meta(j).wait_recv()

    lane = lax.broadcasted_iota(jnp.int32, (8, 128), 1)
    per = 128 // rows
    groups = CORES * nz // per
    slot_row = lax.broadcasted_iota(jnp.int32, (capacity, 128), 0).astype(F32) + 1.0
    slot_lane = lax.broadcasted_iota(jnp.int32, (128, capacity), 1).astype(F32) + 1.0
    sums = [jnp.zeros((capacity, 1), F32) for _ in range(n_exp)]
    for g in range(groups):
        ids = jnp.zeros((8, 128), F32)
        slots = jnp.zeros((8, 128), F32)
        gates = jnp.zeros((8, 128), F32)
        for i in range(per):
            tile = meta_all[g * per + i]
            here = (lane >= i * rows) & (lane < (i + 1) * rows)
            ids = jnp.where(here, pltpu.roll(tile, (i * rows) % 128, 1), ids)
            slots = jnp.where(here, pltpu.roll(tile, ((i - 1) * rows) % 128, 1), slots)
            gates = jnp.where(here, pltpu.roll(tile, ((i - 2) * rows) % 128, 1), gates)
        slot_rows = []
        for e in range(n_exp):
            mine = ids == (me * n_exp + e).astype(F32)
            slot_e = jnp.sum(jnp.where(mine, slots + 1.0, 0.0), axis=0, keepdims=True)
            gate_e = jnp.sum(jnp.where(mine, gates, 0.0), axis=0, keepdims=True)
            hit = slot_row == slot_e
            pick[e * capacity:(e + 1) * capacity, g * 128:(g + 1) * 128] = jnp.where(hit, 1.0, 0.0).astype(BF16)
            sums[e] = sums[e] + jnp.sum(jnp.where(hit, gate_e, 0.0), axis=1, keepdims=True)
            slot_rows.append(slot_e)
        table = jnp.concatenate(slot_rows + [jnp.zeros((8 - n_exp, 128), F32)], axis=0).T
        for e in range(n_exp):
            pick_t[g * 128:(g + 1) * 128, e * capacity:(e + 1) * capacity] = jnp.where(
                slot_lane == table[:, e:e + 1], 1.0, 0.0).astype(BF16)
    for e in range(n_exp):
        slot_gate[e * capacity:(e + 1) * capacity, :] = jnp.broadcast_to(sums[e], (capacity, 128))

    take_tokens(far)
    for j in range(nz):
        for p in range(PIECES):
            die_copy(j, p).wait_recv()

    tok_rows = tok_all.shape[0] * rows

    @pl.loop(0, dim // 512)
    def _(n):
        cols = pl.ds(pl.multiple_of(n * 512, 512), 512)
        block = tok_all[:, :, cols].reshape(tok_rows, 512)
        buf[:, cols] = jnp.dot(pick[...], block, preferred_element_type=F32).astype(BF16)

    @pl.loop(0, n_exp)
    def _(e):
        for copy in gate_copies(e):
            copy.wait()
        here = pl.ds(pl.multiple_of(e * capacity, capacity), capacity)

        @pl.loop(0, ffn // 512)
        def _(n):
            cols = pl.ds(pl.multiple_of(n * 512, 512), 512)
            x = buf[here, :]
            gate_h = jnp.dot(x, wg[e, :, cols], preferred_element_type=F32)
            up_h = jnp.dot(x, wu[e, :, cols], preferred_element_type=F32)
            hid[here, cols] = (jax.nn.silu(gate_h) * up_h).astype(BF16)

    def sum_copy(q):
        return pltpu.make_async_remote_copy(
            die_out.at[lax.rem(q, 2)], die_in.at[q], sum_send.at[lax.rem(q, 2)], sum_recv.at[q],
            device_id=partner, device_id_type=MESH)

    def block_of(way, step):
        return far - step if way == 0 else (far + step) % nz

    def rs_copy(way, kind, q):
        first = slice(0, half) if way == 0 else slice(half, rows)
        second = slice(half, rows) if way == 0 else slice(0, half)
        step, part, dst = ((0, first, ring0), (1, second, ring1), (1, first, ring1),
                           (2, slice(0, rows), ring2), (3, slice(0, rows), ring3))[kind]
        base = block_of(way, step) * rows
        src = acc.at[q, pl.ds(base + part.start, part.stop - part.start), :]
        if kind == 0:
            to = ring0.at[way, q]
        else:
            to = dst.at[way, q, pl.ds(part.start, part.stop - part.start), :]
        return pltpu.make_async_remote_copy(
            src, to, rs_send.at[way, kind, q], rs_recv.at[way, kind, q], device_id=nbr[way], device_id_type=MESH)

    def send_own(q):
        sum_copy(q).wait_recv()
        acc[q] = acc[q] + die_in[q]
        for kind in (0, 1):
            for way in range(2):
                rs_copy(way, kind, q).start()

    @pl.loop(0, n_col)
    def _(q):
        down_copy(q).wait()
        slot = lax.rem(q, DOWN_SLOTS)
        for e in range(n_exp):
            span = slice(e * capacity, (e + 1) * capacity)
            res = jnp.dot(hid[span, :], wd[slot, e], preferred_element_type=F32)
            weights = slot_gate[span, :]
            res = res * jnp.concatenate([weights] * (COLS // 128), axis=1)
            hi = res.astype(BF16)
            rest = res - hi.astype(F32)
            mid = rest.astype(BF16)
            parts[0, span, :] = hi
            parts[1, span, :] = mid
            parts[2, span, :] = (rest - mid.astype(F32)).astype(BF16)

        def added(lo):
            onehot = pick_t[lo:lo + side, :]
            return (jnp.dot(onehot, parts[0], preferred_element_type=F32)
                    + jnp.dot(onehot, parts[1], preferred_element_type=F32)
                    + jnp.dot(onehot, parts[2], preferred_element_type=F32))

        @pl.when(q >= 2)
        def _():
            sum_copy(q - 2).wait_send()

        die_out[lax.rem(q, 2)] = added(side)
        sum_copy(q).start()
        acc[q] = added(0)

        @pl.when(q + DOWN_SLOTS < n_col)
        def _():
            down_copy(q + DOWN_SLOTS).start(priority=1)

        @pl.when(q >= 1)
        def _():
            send_own(q - 1)

    send_own(n_col - 1)

    @pl.loop(0, n_col)
    def _(q):
        for way in range(2):
            rs_copy(way, 0, q).wait_recv()
            lo = block_of(way, 1) * rows + (0 if way == 0 else half)
            acc[q, lo:lo + half, :] = acc[q, lo:lo + half, :] + ring0[way, q]
            rs_copy(way, 2, q).start()

    for step, ring, kinds in ((2, ring1, (1, 2)), (3, ring2, (3,))):
        @pl.loop(0, n_col)
        def _(q):
            for way in range(2):
                for kind in kinds:
                    rs_copy(way, kind, q).wait_recv()
                lo = block_of(way, step) * rows
                acc[q, lo:lo + rows, :] = acc[q, lo:lo + rows, :] + ring[way, q]
                rs_copy(way, step + 1, q).start()

    @pl.loop(0, n_col)
    def _(q):
        for way in range(2):
            rs_copy(way, 4, q).wait_recv()
        cols = pl.ds(pl.multiple_of(q * COLS, COLS), COLS)
        out_ref[:, cols] = (acc[q, 0:rows, :] + (ring3[0, q] + ring3[1, q])).astype(out_ref.dtype)

    for way in range(2):
        for hop in range(1, far + 1):
            if meta_on_ring(way, hop):
                ring_meta(way, hop).wait_send()
            for p in range(PIECES):
                if on_ring(way, hop, p):
                    ring_copy(way, hop, p).wait_send()
    for j in range(nz):
        die_meta(j).wait_send()
        for p in range(PIECES):
            die_copy(j, p).wait_send()
    for q in range(max(n_col - 2, 0), n_col):
        sum_copy(q).wait_send()

    @pl.loop(0, n_col)
    def _(q):
        for way in range(2):
            for kind in range(5):
                rs_copy(way, kind, q).wait_send()


def solution(mesh):
    row_spec = P(('dp', 'ep'), None)
    exp_spec = P('ep', None, None)
    devs = mesh.shape['ep']
    nz = devs // CORES

    def local_moe(tok_rows, expert_ids, gate_weights, slot_ids, w_gate, w_up, w_down):
        rows, dim = tok_rows.shape
        top_k = expert_ids.shape[1]
        n_exp, _, ffn = w_gate.shape
        capacity = 2 * top_k * rows // n_exp
        n_col = dim // COLS
        far = nz // 2
        slots = n_exp * capacity
        total = devs * rows
        dma = pltpu.SemaphoreType.DMA
        vmem = pltpu.VMEM
        scratch = [
            vmem((devs, rows, dim), BF16), vmem((devs, 8, 128), F32),
            vmem((n_exp, dim, ffn), BF16), vmem((n_exp, dim, ffn), BF16),
            vmem((min(DOWN_SLOTS, n_col), n_exp, ffn, COLS), BF16),
            vmem((slots, total), BF16), vmem((total, slots), BF16), vmem((slots, 128), F32),
            vmem((slots, dim), BF16), vmem((slots, ffn), BF16), vmem((3, slots, COLS), BF16),
            vmem((n_col, nz * rows, COLS), F32), vmem((2, nz * rows, COLS), F32), vmem((n_col, nz * rows, COLS), F32),
            vmem((2, n_col, rows // 2, COLS), F32),
            vmem((2, n_col, rows, COLS), F32), vmem((2, n_col, rows, COLS), F32), vmem((2, n_col, rows, COLS), F32),
            dma, dma((n_exp, 2)), dma((n_col,)),
            dma((2, far, PIECES)), dma((2, far, PIECES)), dma((2, far)), dma((2, far)),
            dma((nz, PIECES)), dma((nz, PIECES)), dma((nz,)), dma((nz,)),
            dma((2,)), dma((n_col,)),
            dma((2, 5, n_col)), dma((2, 5, n_col)),
        ]
        anyspace = pl.BlockSpec(memory_space=pl.ANY)
        in_vmem = pl.BlockSpec(memory_space=pltpu.VMEM)
        flops = 6 * slots * dim * ffn
        return pl.pallas_call(
            functools.partial(moe_kernel, nz, capacity),
            out_shape=jax.ShapeDtypeStruct((rows, dim), tok_rows.dtype),
            in_specs=[anyspace, in_vmem, in_vmem, in_vmem, anyspace, anyspace, anyspace],
            out_specs=in_vmem,
            scratch_shapes=scratch,
            name='routed_experts',
            cost_estimate=pl.CostEstimate(flops=flops, bytes_accessed=6 * n_exp * dim * ffn, transcendentals=slots * ffn),
            compiler_params=pltpu.CompilerParams(
                collective_id=0, has_side_effects=True, vmem_limit_bytes=67043328),
        )(tok_rows, expert_ids.T, slot_ids.T, gate_weights.T, w_gate, w_up, w_down)

    return jax.shard_map(local_moe, mesh=mesh, in_specs=(row_spec, row_spec, row_spec, row_spec, exp_spec, exp_spec, exp_spec), out_specs=row_spec, check_vma=False)
```

time: 208 us -> 69.6 us (0.33); the launches traced: 205 us -> 69.5 us
  Pallas kernels: 0 us -> 67.9 us
  waiting for transfers between devices: 55.4 us -> 0 us
  blocking collectives: 53.8 us -> 0 us
  local copies, waits for them, and re-layouts: 38.2 us -> 1.57 us
  matrix products: 27.4 us -> 0 us
  other arithmetic: 17 us -> 0 us
  between operations: 13.5 us -> 0.01 us
    pallas_call x0 -> x1, Pallas kernels: none -> 67.9 us  [local_moe(): pl.pallas_call(functools.partial(moe_kernel, nz, capacity), out_shape=jax...]
    reduce_scatter x1 -> x0, waiting for transfers between devices: 54.6 us -> none  [local_moe(): summed = lax.psum_scatter(partial, 'ep', scatter_dimension=0, tiled=True)]
    all_gather x3 -> x0, blocking collectives: 53.8 us -> none  [the longest x1 22.9 us: local_moe(): all_ids = lax.all_gather(expert_ids, 'ep', tiled=True)]
    scatter x2 -> x0, local copies, waits for them, and re-layouts: 31.2 us -> none  [the longest x1 15.7 us: local_moe(): jnp.full((num_rows,), group_rows, jnp.int32).at[flat_ids]]
    dot_general x2 -> x0, matrix products: 27.4 us -> none  [the longest x1 17.9 us: local_moe(): jnp.einsum('ecf,efd->ecd', hidden, w_down, preferred_element_type=jnp.flo...]
    scatter-add x1 -> x0, other arithmetic: 10.8 us -> none  [local_moe(): jnp.zeros((group_rows, model_dim), jnp.float32).at[src_rows]]
    gather x1 -> x0, local copies, waits for them, and re-layouts: 6.27 us -> none  [local_moe(): jnp.take(all_tok, src_rows, axis=0, mode='fill', fill_value=0)]
    mul x1 -> x0, other arithmetic: 4.49 us -> none  [local_moe(): weighted = exp_out.reshape(num_rows, model_dim) * gate_rows[:, None]]
  transfers between devices with their start and end apart: 2 -> 0, of which waited for: 1 -> 0; matrix products, arithmetic and copies ran while one was open for 16% -> 0% of each run, Pallas kernels for 0% -> 0%
where the time goes in v1:
time: 69.6 us; the launch traced here: 69.5 us
  Pallas kernels  67.9 us (98%)
  local copies, waits for them, and re-layouts  1.57 us (2%)
    pallas_call x1, Pallas kernels, local_moe(): pl.pallas_call(functools.partial(moe_kernel, nz, capacity), out_shape=jax...  67.9 us
    unnamed x1, local copies, waits for them, and re-layouts  1.57 us

profile of v1, /device:TPU:21, one launch (start us, length us, event | category | flops | bytes accessed | tf_op | source)
XLA Modules:
  0.0 69.5 jit_solution(6304957425211077365)
XLA Ops:
  0.0 67.9 %routed_experts.1 = bf16[32,2048]{1,0:T(8,128)(2,1)} custom-call(bf16[32,2048]{1,0:T(8,128)(2,1)} %tok_hbm.1, s32[8,32]{1,0:T(8,128)} %bitcast.3, s32[8,32]{1,0:T(8,128)} %bitcast.4, f32[8,32]{1,0:T(8,128)} %bitcast.5, bf16[4,2048,1024]{2,1,0:T(8,128)(2,1)} %wg_hbm.1, bf16[4,2048,1024]{2,1,0:T(8,128)(2,1)} %wu_hbm.1, bf16[4,1024,2048]{2,1,0:T(8,128)(2,1)} %wd_hbm.1), custom_call_target="tpu_custom_call" | custom-call | flops 6442450944 | bytes 50331648 | tf_op jit(solution)/shard_map/routed_experts/pallas_call | solution.py:345
  67.9 1.6 %copy.9 = bf16[32,2048]{1,0:T(8,128)(2,1)} copy(bf16[32,2048]{1,0:T(8,128)(2,1)} %routed_experts.1) | data formatting | bytes 262144

commit v2 on v1

--- a/solution.py
+++ b/solution.py
@@ -16,10 +16,10 @@
 BF16 = jnp.bfloat16
 
 
-def moe_kernel(nz, capacity, tok_hbm, ids_ref, slots_ref, gates_ref, wg_hbm, wu_hbm, wd_hbm, out_ref,
-               tok_all, meta_all, wg, wu, wd, pick, pick_t, slot_gate, buf, hid, parts,
+def moe_kernel(nz, capacity, tok_hbm, ids_hbm, slots_hbm, gates_hbm, wg_hbm, wu_hbm, wd_hbm, out_ref,
+               ids_ref, slots_ref, gates_ref, tok_all, meta_all, wg, wu, wd, pick, pick_t, slot_gate, buf, hid, parts_a, parts_b,
                acc, die_out, die_in, ring0, ring1, ring2, ring3,
-               in_sem, gate_sem, down_sem, ag_send, ag_recv, agm_send, agm_recv, die_send, die_recv,
+               in_sem, route_sem, gate_sem, down_sem, ag_send, ag_recv, agm_send, agm_recv, die_send, die_recv,
                diem_send, diem_recv, sum_send, sum_recv, rs_send, rs_recv):
     rows = tok_hbm.shape[0]
     dim = tok_hbm.shape[1]
@@ -37,8 +37,15 @@
     nbr = (right, left)
     piece = dim // PIECES
 
+    barrier = pltpu.get_barrier_semaphore()
+    for dev in (right, left, partner):
+        pl.semaphore_signal(barrier, inc=1, device_id=dev, device_id_type=MESH)
     own = pltpu.make_async_copy(tok_hbm, tok_all.at[0], in_sem)
     own.start()
+    routes = [pltpu.make_async_copy(src, dst, route_sem.at[i]) for i, (src, dst) in enumerate(
+        ((ids_hbm, ids_ref), (slots_hbm, slots_ref), (gates_hbm, gates_ref)))]
+    for copy in routes:
+        copy.start()
 
     def gate_copies(e):
         return (pltpu.make_async_copy(wg_hbm.at[e], wg.at[e], gate_sem.at[e, 0]),
@@ -54,16 +61,24 @@
     for q in range(min(DOWN_SLOTS, n_col)):
         down_copy(q).start(priority=1)
 
-    barrier = pltpu.get_barrier_semaphore()
-    for dev in (right, left, partner):
-        pl.semaphore_signal(barrier, inc=1, device_id=dev, device_id_type=MESH)
-
+    for copy in routes:
+        copy.wait()
     meta_all[0] = jnp.concatenate(
         [ids_ref[...].astype(F32), slots_ref[...].astype(F32), gates_ref[...],
          jnp.zeros(gates_ref.shape, F32)], axis=1)
     pl.semaphore_wait(barrier, 3)
     own.wait()
 
+    order = [0]
+    for hop in range(1, far):
+        order += [hop, nz - hop]
+    order.append(far)
+    place = {j: order.index(j) for j in range(nz)}
+    quad = nz // 2
+
+    def spot(other, j):
+        return (place[j] // quad) * nz + other * quad + place[j] % quad
+
     def cols_of(p):
         return pl.ds(p * piece, piece)
 
@@ -71,24 +86,24 @@
         src = (nz - hop + 1) % nz if way == 0 else hop - 1
         dst = nz - hop if way == 0 else hop
         return pltpu.make_async_remote_copy(
-            tok_all.at[src, :, cols_of(p)], tok_all.at[dst, :, cols_of(p)],
+            tok_all.at[spot(0, src), :, cols_of(p)], tok_all.at[spot(0, dst), :, cols_of(p)],
             ag_send.at[way, hop - 1, p], ag_recv.at[way, hop - 1, p], device_id=nbr[way], device_id_type=MESH)
 
     def ring_meta(way, hop):
         src = (nz - hop + 1) % nz if way == 0 else hop - 1
         dst = nz - hop if way == 0 else hop
         return pltpu.make_async_remote_copy(
-            meta_all.at[src], meta_all.at[dst], agm_send.at[way, hop - 1], agm_recv.at[way, hop - 1],
+            meta_all.at[spot(0, src)], meta_all.at[spot(0, dst)], agm_send.at[way, hop - 1], agm_recv.at[way, hop - 1],
             device_id=nbr[way], device_id_type=MESH)
 
     def die_copy(j, p):
         return pltpu.make_async_remote_copy(
-            tok_all.at[j, :, cols_of(p)], tok_all.at[nz + j, :, cols_of(p)],
+            tok_all.at[spot(0, j), :, cols_of(p)], tok_all.at[spot(1, j), :, cols_of(p)],
             die_send.at[j, p], die_recv.at[j, p], device_id=partner, device_id_type=MESH)
 
     def die_meta(j):
         return pltpu.make_async_remote_copy(
-            meta_all.at[j], meta_all.at[nz + j], diem_send.at[j], diem_recv.at[j],
+            meta_all.at[spot(0, j)], meta_all.at[spot(1, j)], diem_send.at[j], diem_recv.at[j],
             device_id=partner, device_id_type=MESH)
 
     def on_ring(way, hop, p):
@@ -126,20 +141,12 @@
                         ring_copy(way, hop + 1, p).start()
                     die_copy(nz - hop if way == 0 else hop, p).start()
 
-    for hop in range(1, far):
-        take_meta(hop)
-        take_tokens(hop)
-    take_meta(far)
-    for j in range(nz):
-        die_meta(j).wait_recv()
-
     lane = lax.broadcasted_iota(jnp.int32, (8, 128), 1)
     per = 128 // rows
-    groups = CORES * nz // per
     slot_row = lax.broadcasted_iota(jnp.int32, (capacity, 128), 0).astype(F32) + 1.0
     slot_lane = lax.broadcasted_iota(jnp.int32, (128, capacity), 1).astype(F32) + 1.0
-    sums = [jnp.zeros((capacity, 1), F32) for _ in range(n_exp)]
-    for g in range(groups):
+
+    def one_hots(g):
         ids = jnp.zeros((8, 128), F32)
         slots = jnp.zeros((8, 128), F32)
         gates = jnp.zeros((8, 128), F32)
@@ -155,38 +162,58 @@
             slot_e = jnp.sum(jnp.where(mine, slots + 1.0, 0.0), axis=0, keepdims=True)
             gate_e = jnp.sum(jnp.where(mine, gates, 0.0), axis=0, keepdims=True)
             hit = slot_row == slot_e
-            pick[e * capacity:(e + 1) * capacity, g * 128:(g + 1) * 128] = jnp.where(hit, 1.0, 0.0).astype(BF16)
-            sums[e] = sums[e] + jnp.sum(jnp.where(hit, gate_e, 0.0), axis=1, keepdims=True)
+            span = slice(e * capacity, (e + 1) * capacity)
+            pick[span, g * 128:(g + 1) * 128] = jnp.where(hit, 1.0, 0.0).astype(BF16)
+            gate_sum = jnp.broadcast_to(jnp.sum(jnp.where(hit, gate_e, 0.0), axis=1, keepdims=True), (capacity, 128))
+            slot_gate[span, :] = gate_sum if g == 0 else slot_gate[span, :] + gate_sum
             slot_rows.append(slot_e)
         table = jnp.concatenate(slot_rows + [jnp.zeros((8 - n_exp, 128), F32)], axis=0).T
+        base = ((g % 2) * 2 + g // 2) * 128
         for e in range(n_exp):
-            pick_t[g * 128:(g + 1) * 128, e * capacity:(e + 1) * capacity] = jnp.where(
+            pick_t[base:base + 128, e * capacity:(e + 1) * capacity] = jnp.where(
                 slot_lane == table[:, e:e + 1], 1.0, 0.0).astype(BF16)
-    for e in range(n_exp):
-        slot_gate[e * capacity:(e + 1) * capacity, :] = jnp.broadcast_to(sums[e], (capacity, 128))
-
+
+    def gather(part):
+        @pl.loop(0, dim // 512)
+        def _(n):
+            cols = pl.ds(pl.multiple_of(n * 512, 512), 512)
+            block = tok_all[part * nz:(part + 1) * nz, :, cols].reshape(nz * rows, 512)
+            got = jnp.dot(pick[:, part * nz * rows:(part + 1) * nz * rows], block, preferred_element_type=F32)
+            if part == 0:
+                buf[:, cols] = got.astype(BF16)
+            else:
+                buf[:, cols] = (buf[:, cols].astype(F32) + got).astype(BF16)
+
+    def die_ready(blocks):
+        for j in blocks:
+            for p in range(PIECES):
+                die_copy(j, p).wait_recv()
+
+    for hop in range(1, far):
+        take_meta(hop)
+        take_tokens(hop)
+    for j in order[:quad]:
+        die_meta(j).wait_recv()
+    one_hots(0)
+    one_hots(1)
+    die_ready(order[:quad])
+    gather(0)
+    take_meta(far)
+    for j in order[quad:]:
+        die_meta(j).wait_recv()
+    one_hots(2)
+    one_hots(3)
     take_tokens(far)
-    for j in range(nz):
-        for p in range(PIECES):
-            die_copy(j, p).wait_recv()
-
-    tok_rows = tok_all.shape[0] * rows
-
-    @pl.loop(0, dim // 512)
-    def _(n):
-        cols = pl.ds(pl.multiple_of(n * 512, 512), 512)
-        block = tok_all[:, :, cols].reshape(tok_rows, 512)
-        buf[:, cols] = jnp.dot(pick[...], block, preferred_element_type=F32).astype(BF16)
+    die_ready(order[quad:])
+    gather(1)
 
     @pl.loop(0, n_exp)
     def _(e):
         for copy in gate_copies(e):
             copy.wait()
         here = pl.ds(pl.multiple_of(e * capacity, capacity), capacity)
-
-        @pl.loop(0, ffn // 512)
-        def _(n):
-            cols = pl.ds(pl.multiple_of(n * 512, 512), 512)
+        for n in range(ffn // 512):
+            cols = slice(n * 512, (n + 1) * 512)
             x = buf[here, :]
             gate_h = jnp.dot(x, wg[e, :, cols], preferred_element_type=F32)
             up_h = jnp.dot(x, wu[e, :, cols], preferred_element_type=F32)
@@ -205,7 +232,7 @@
         second = slice(half, rows) if way == 0 else slice(0, half)
         step, part, dst = ((0, first, ring0), (1, second, ring1), (1, first, ring1),
                            (2, slice(0, rows), ring2), (3, slice(0, rows), ring3))[kind]
-        base = block_of(way, step) * rows
+        base = place[block_of(way, step)] * rows
         src = acc.at[q, pl.ds(base + part.start, part.stop - part.start), :]
         if kind == 0:
             to = ring0.at[way, q]
@@ -221,42 +248,43 @@
             for way in range(2):
                 rs_copy(way, kind, q).start()
 
-    @pl.loop(0, n_col)
-    def _(q):
-        down_copy(q).wait()
-        slot = lax.rem(q, DOWN_SLOTS)
+    parts = (parts_a, parts_b)
+
+    def project(q):
+        into = parts[q % 2]
         for e in range(n_exp):
             span = slice(e * capacity, (e + 1) * capacity)
-            res = jnp.dot(hid[span, :], wd[slot, e], preferred_element_type=F32)
-            weights = slot_gate[span, :]
-            res = res * jnp.concatenate([weights] * (COLS // 128), axis=1)
+            res = jnp.dot(hid[span, :], wd[q % DOWN_SLOTS, e], preferred_element_type=F32)
+            res = res * jnp.concatenate([slot_gate[span, :]] * (COLS // 128), axis=1)
             hi = res.astype(BF16)
             rest = res - hi.astype(F32)
             mid = rest.astype(BF16)
-            parts[0, span, :] = hi
-            parts[1, span, :] = mid
-            parts[2, span, :] = (rest - mid.astype(F32)).astype(BF16)
-
-        def added(lo):
-            onehot = pick_t[lo:lo + side, :]
-            return (jnp.dot(onehot, parts[0], preferred_element_type=F32)
-                    + jnp.dot(onehot, parts[1], preferred_element_type=F32)
-                    + jnp.dot(onehot, parts[2], preferred_element_type=F32))
-
-        @pl.when(q >= 2)
-        def _():
+            into[0, span, :] = hi
+            into[1, span, :] = mid
+            into[2, span, :] = (rest - mid.astype(F32)).astype(BF16)
+
+    def added(q, lo):
+        onehot = pick_t[lo:lo + side, :]
+        part = parts[q % 2]
+        return (jnp.dot(onehot, part[0], preferred_element_type=F32)
+                + jnp.dot(onehot, part[1], preferred_element_type=F32)
+                + jnp.dot(onehot, part[2], preferred_element_type=F32))
+
+    down_copy(0).wait()
+    project(0)
+    for q in range(n_col):
+        if q + 1 < n_col:
+            down_copy(q + 1).wait()
+        if q >= 2:
             sum_copy(q - 2).wait_send()
-
-        die_out[lax.rem(q, 2)] = added(side)
+        die_out[q % 2] = added(q, side)
+        acc[q] = added(q, 0)
+        if q + 1 < n_col:
+            project(q + 1)
         sum_copy(q).start()
-        acc[q] = added(0)
-
-        @pl.when(q + DOWN_SLOTS < n_col)
-        def _():
+        if q + DOWN_SLOTS < n_col:
             down_copy(q + DOWN_SLOTS).start(priority=1)
-
-        @pl.when(q >= 1)
-        def _():
+        if q >= 1:
             send_own(q - 1)
 
     send_own(n_col - 1)
@@ -265,7 +293,7 @@
     def _(q):
         for way in range(2):
             rs_copy(way, 0, q).wait_recv()
-            lo = block_of(way, 1) * rows + (0 if way == 0 else half)
+            lo = place[block_of(way, 1)] * rows + (0 if way == 0 else half)
             acc[q, lo:lo + half, :] = acc[q, lo:lo + half, :] + ring0[way, q]
             rs_copy(way, 2, q).start()
 
@@ -275,7 +303,7 @@
             for way in range(2):
                 for kind in kinds:
                     rs_copy(way, kind, q).wait_recv()
-                lo = block_of(way, step) * rows
+                lo = place[block_of(way, step)] * rows
                 acc[q, lo:lo + rows, :] = acc[q, lo:lo + rows, :] + ring[way, q]
                 rs_copy(way, step + 1, q).start()
 
@@ -325,15 +353,16 @@
         dma = pltpu.SemaphoreType.DMA
         vmem = pltpu.VMEM
         scratch = [
+            vmem((top_k, rows), jnp.int32), vmem((top_k, rows), jnp.int32), vmem((top_k, rows), F32),
             vmem((devs, rows, dim), BF16), vmem((devs, 8, 128), F32),
             vmem((n_exp, dim, ffn), BF16), vmem((n_exp, dim, ffn), BF16),
             vmem((min(DOWN_SLOTS, n_col), n_exp, ffn, COLS), BF16),
             vmem((slots, total), BF16), vmem((total, slots), BF16), vmem((slots, 128), F32),
-            vmem((slots, dim), BF16), vmem((slots, ffn), BF16), vmem((3, slots, COLS), BF16),
+            vmem((slots, dim), BF16), vmem((slots, ffn), BF16), vmem((3, slots, COLS), BF16), vmem((3, slots, COLS), BF16),
             vmem((n_col, nz * rows, COLS), F32), vmem((2, nz * rows, COLS), F32), vmem((n_col, nz * rows, COLS), F32),
             vmem((2, n_col, rows // 2, COLS), F32),
             vmem((2, n_col, rows, COLS), F32), vmem((2, n_col, rows, COLS), F32), vmem((2, n_col, rows, COLS), F32),
-            dma, dma((n_exp, 2)), dma((n_col,)),
+            dma, dma((3,)), dma((n_exp, 2)), dma((n_col,)),
             dma((2, far, PIECES)), dma((2, far, PIECES)), dma((2, far)), dma((2, far)),
             dma((nz, PIECES)), dma((nz, PIECES)), dma((nz,)), dma((nz,)),
             dma((2,)), dma((n_col,)),
@@ -345,7 +374,7 @@
         return pl.pallas_call(
             functools.partial(moe_kernel, nz, capacity),
             out_shape=jax.ShapeDtypeStruct((rows, dim), tok_rows.dtype),
-            in_specs=[anyspace, in_vmem, in_vmem, in_vmem, anyspace, anyspace, anyspace],
+            in_specs=[anyspace] * 7,
             out_specs=in_vmem,
             scratch_shapes=scratch,
             name='routed_experts',

time: 69.6 us -> 64.8 us (0.931)
  Pallas kernels: 67.9 us -> 63.2 us
    pallas_call x1, Pallas kernels: 67.9 us -> 63.2 us  [local_moe(): pl.pallas_call(functools.partial(moe_kernel, nz, capacity), out_shape=jax...]
where the time goes in v2:
time: 64.8 us; the launch traced here: 64.7 us
  Pallas kernels  63.2 us (98%)
  local copies, waits for them, and re-layouts  1.57 us (2%)
    pallas_call x1, Pallas kernels, local_moe(): pl.pallas_call(functools.partial(moe_kernel, nz, capacity), out_shape=jax...  63.2 us
    unnamed x1, local copies, waits for them, and re-layouts  1.57 us

profile of v2, /device:TPU:21, one launch (start us, length us, event | category | flops | bytes accessed | tf_op | source)
XLA Modules:
  0.0 64.7 jit_solution(11882435412590495350)
XLA Ops:
  0.0 63.2 %routed_experts.1 = bf16[32,2048]{1,0:T(8,128)(2,1)} custom-call(bf16[32,2048]{1,0:T(8,128)(2,1)} %tok_hbm.1, s32[8,32]{1,0:T(8,128)} %bitcast.3, s32[8,32]{1,0:T(8,128)} %bitcast.4, f32[8,32]{1,0:T(8,128)} %bitcast.5, bf16[4,2048,1024]{2,1,0:T(8,128)(2,1)} %wg_hbm.1, bf16[4,2048,1024]{2,1,0:T(8,128)(2,1)} %wu_hbm.1, bf16[4,1024,2048]{2,1,0:T(8,128)(2,1)} %wd_hbm.1), custom_call_target="tpu_custom_call" | custom-call | flops 6442450944 | bytes 50331648 | tf_op jit(solution)/shard_map/routed_experts/pallas_call | solution.py:374
  63.2 1.6 %copy.9 = bf16[32,2048]{1,0:T(8,128)(2,1)} copy(bf16[32,2048]{1,0:T(8,128)(2,1)} %routed_experts.1) | data formatting | bytes 262144

commit v3 on v0

v3 whole, which is shorter than its diff:
```python
import functools

import jax
import jax.numpy as jnp
from jax import lax
from jax.experimental import pallas as pl
from jax.experimental.pallas import tpu as pltpu
from jax.sharding import PartitionSpec as P

CORES = 2
HALVES = 2
PIECES = 2
COLS = 512
MESH = pl.DeviceIdType.MESH
F32 = jnp.float32
BF16 = jnp.bfloat16


def moe_kernel(nz, capacity, tok_hbm, ids_hbm, slots_hbm, gates_hbm, wg_hbm, wu_hbm, wd_hbm, out_ref,
               ids_ref, slots_ref, gates_ref, tok, meta_all, wg, wu, wd, pick, pick_t, slot_gate, buf, hid,
               parts_a, parts_b, acc, die_out, die_in, ring0, ring1, ring2, ring3,
               in_sem, route_sem, gate_sem, down_sem, ag_send, ag_recv, agm_send, agm_recv, die_send, die_recv,
               diem_send, diem_recv, sum_send, sum_recv, rs_send, rs_recv):
    rows, dim = tok_hbm.shape
    n_exp, _, ffn = wg.shape
    n_col = dim // COLS
    hr = rows // HALVES
    far = nz // 2
    side = nz * hr
    me = lax.axis_index('ep')
    z = me // CORES
    core = me % CORES
    right = {'ep': ((z + 1) % nz) * CORES + core}
    left = {'ep': ((z + nz - 1) % nz) * CORES + core}
    partner = {'ep': z * CORES + (1 - core)}
    nbr = (right, left)
    piece = dim // PIECES

    barrier = pltpu.get_barrier_semaphore()
    for dev in (right, left, partner):
        pl.semaphore_signal(barrier, inc=1, device_id=dev, device_id_type=MESH)

    def own_copy(h):
        return pltpu.make_async_copy(tok_hbm.at[h * hr:(h + 1) * hr], tok.at[h, 0], in_sem.at[h])

    routes = [pltpu.make_async_copy(src, dst, route_sem.at[i]) for i, (src, dst) in enumerate(
        ((ids_hbm, ids_ref), (slots_hbm, slots_ref), (gates_hbm, gates_ref)))]
    for copy in routes:
        copy.start()
    for h in range(HALVES):
        own_copy(h).start()

    def gate_copies(e):
        return (pltpu.make_async_copy(wg_hbm.at[e], wg.at[e], gate_sem.at[e, 0]),
                pltpu.make_async_copy(wu_hbm.at[e], wu.at[e], gate_sem.at[e, 1]))

    def down_copy(q):
        return pltpu.make_async_copy(wd_hbm.at[:, :, q * COLS:(q + 1) * COLS], wd.at[q], down_sem.at[q])

    for e in range(n_exp):
        for copy in gate_copies(e):
            copy.start(priority=1)
    for q in range(n_col):
        down_copy(q).start(priority=1)

    for copy in routes:
        copy.wait()
    meta_all[0] = jnp.concatenate(
        [ids_ref[...].astype(F32), slots_ref[...].astype(F32), gates_ref[...],
         jnp.zeros(gates_ref.shape, F32)], axis=1)
    for h in range(HALVES):
        own_copy(h).wait()
    pl.semaphore_wait(barrier, 3)

    def ends(way, hop):
        return ((nz - hop + 1) % nz, nz - hop) if way == 0 else (hop - 1, hop)

    def ring_copy(h, way, hop, p):
        src, dst = ends(way, hop)
        cols = pl.ds(p * piece, piece)
        return pltpu.make_async_remote_copy(
            tok.at[h, src, :, cols], tok.at[h, dst, :, cols],
            ag_send.at[h, way, hop - 1, p], ag_recv.at[h, way, hop - 1, p], device_id=nbr[way], device_id_type=MESH)

    def ring_meta(way, hop):
        src, dst = ends(way, hop)
        return pltpu.make_async_remote_copy(
            meta_all.at[src], meta_all.at[dst], agm_send.at[way, hop - 1], agm_recv.at[way, hop - 1],
            device_id=nbr[way], device_id_type=MESH)

    def die_copy(h, j, p):
        cols = pl.ds(p * piece, piece)
        return pltpu.make_async_remote_copy(
            tok.at[h, j, :, cols], tok.at[h, nz + j, :, cols],
            die_send.at[h, j, p], die_recv.at[h, j, p], device_id=partner, device_id_type=MESH)

    def die_meta(j):
        return pltpu.make_async_remote_copy(
            meta_all.at[j], meta_all.at[nz + j], diem_send.at[j], diem_recv.at[j],
            device_id=partner, device_id_type=MESH)

    def on_ring(way, hop, p):
        return hop < far or (hop == far and (p < PIECES // 2) == (way == 0))

    def meta_on_ring(way, hop):
        return hop < far or (hop == far and way == 0)

    def take_meta(hop):
        for way in range(2):
            if meta_on_ring(way, hop):
                ring_meta(way, hop).wait_recv()
                if meta_on_ring(way, hop + 1):
                    ring_meta(way, hop + 1).start()
                die_meta(ends(way, hop)[1]).start()

    def send_own_block(h, p):
        for way in range(2):
            ring_copy(h, way, 1, p).start()
        die_copy(h, 0, p).start()

    def take_block(h, hop, p):
        for way in range(2):
            if on_ring(way, hop, p):
                ring_copy(h, way, hop, p).wait_recv()
                if on_ring(way, hop + 1, p):
                    ring_copy(h, way, hop + 1, p).start()
                die_copy(h, ends(way, hop)[1], p).start()

    def take_blocks(h, hop):
        for p in range(PIECES):
            take_block(h, hop, p)

    def die_ready(h):
        for j in range(nz):
            for p in range(PIECES):
                die_copy(h, j, p).wait_recv()

    lane = lax.broadcasted_iota(jnp.int32, (8, 128), 1)
    slot_row = lax.broadcasted_iota(jnp.int32, (capacity, 128), 0).astype(F32) + 1.0
    slot_lane = lax.broadcasted_iota(jnp.int32, (128, capacity), 1).astype(F32) + 1.0

    def one_hots(h, other, picks, sums_too):
        ids = jnp.zeros((8, 128), F32)
        slots = jnp.zeros((8, 128), F32)
        gates = jnp.zeros((8, 128), F32)
        for j in range(nz):
            tile = meta_all[other * nz + j]
            here = (lane >= j * hr) & (lane < (j + 1) * hr)
            shift = (j - h) * hr
            ids = jnp.where(here, pltpu.roll(tile, shift % 128, 1), ids)
            slots = jnp.where(here, pltpu.roll(tile, (shift - rows) % 128, 1), slots)
            gates = jnp.where(here, pltpu.roll(tile, (shift - 2 * rows) % 128, 1), gates)
        slot_rows = []
        base = other * 128
        for e in range(n_exp):
            mine = ids == (me * n_exp + e).astype(F32)
            slot_e = jnp.sum(jnp.where(mine, slots + 1.0, 0.0), axis=0, keepdims=True)
            gate_e = jnp.sum(jnp.where(mine, gates, 0.0), axis=0, keepdims=True)
            hit = slot_row == slot_e
            span = slice(e * capacity, (e + 1) * capacity)
            if picks:
                pick[span, base:base + 128] = jnp.where(hit, 1.0, 0.0).astype(BF16)
            if sums_too:
                gate_sum = jnp.broadcast_to(
                    jnp.sum(jnp.where(hit, gate_e, 0.0), axis=1, keepdims=True), (capacity, 128))
                slot_gate[span, :] = gate_sum if h + other == 0 else slot_gate[span, :] + gate_sum
            slot_rows.append(slot_e)
        if not sums_too:
            return
        table = jnp.concatenate(slot_rows + [jnp.zeros((8 - n_exp, 128), F32)], axis=0).T
        for e in range(n_exp):
            pick_t[h, base:base + 128, e * capacity:(e + 1) * capacity] = jnp.where(
                slot_lane == table[:, e:e + 1], 1.0, 0.0).astype(BF16)

    def gather(h):
        for n in range(dim // 512):
            cols = slice(n * 512, (n + 1) * 512)
            block = tok[h, :, :, cols].reshape(CORES * side, 512)
            buf[:, cols] = jnp.dot(pick[...], block, preferred_element_type=F32).astype(BF16)

    def gate_up(e, n):
        span = slice(e * capacity, (e + 1) * capacity)
        cols = slice(n * 512, (n + 1) * 512)
        x = buf[span, :]
        gate_h = jnp.dot(x, wg[e, :, cols], preferred_element_type=F32)
        up_h = jnp.dot(x, wu[e, :, cols], preferred_element_type=F32)
        hid[span, cols] = (jax.nn.silu(gate_h) * up_h).astype(BF16)

    parts = (parts_a, parts_b)

    def project(h, q):
        into = parts[q % 2]
        for e in range(n_exp):
            span = slice(e * capacity, (e + 1) * capacity)
            res = jnp.dot(hid[span, :], wd[q, e], preferred_element_type=F32)
            res = res * jnp.concatenate([slot_gate[span, :]] * (COLS // 128), axis=1)
            hi = res.astype(BF16)
            rest = res - hi.astype(F32)
            mid = rest.astype(BF16)
            into[0, span, :] = hi
            into[1, span, :] = mid
            into[2, span, :] = (rest - mid.astype(F32)).astype(BF16)

    def added(h, q, other):
        onehot = pick_t[h, other * side:(other + 1) * side, :]
        part = parts[q % 2]
        return (jnp.dot(onehot, part[0], preferred_element_type=F32)
                + jnp.dot(onehot, part[1], preferred_element_type=F32)
                + jnp.dot(onehot, part[2], preferred_element_type=F32))

    def sum_copy(h, q):
        return pltpu.make_async_remote_copy(
            die_out.at[q % 2], die_in.at[h, q], sum_send.at[h, q], sum_recv.at[h, q],
            device_id=partner, device_id_type=MESH)

    def block_of(way, step):
        return far - step if way == 0 else (far + step) % nz

    def rows_of(way, step, kind):
        base = block_of(way, step) * hr
        if kind == 'all':
            return base, hr
        return base + (hr // 2 if (kind == 'first') == (way == 1) else 0), hr // 2

    def rs_copy(h, way, kind, q):
        step, part, dst = ((0, 'first', ring0), (1, 'second', ring1), (1, 'first', ring1),
                           (2, 'all', ring2), (3, 'all', ring3))[kind]
        lo, size = rows_of(way, step, part)
        src = acc.at[h, q, pl.ds(lo, size), :]
        to = dst.at[h, way, q, pl.ds(0 if kind == 0 else lo - block_of(way, step) * hr, size), :]
        return pltpu.make_async_remote_copy(
            src, to, rs_send.at[h, way, kind, q], rs_recv.at[h, way, kind, q], device_id=nbr[way], device_id_type=MESH)

    def own_sums(h, q):
        sum_copy(h, q).wait_recv()
        acc[h, q] = acc[h, q] + die_in[h, q]
        for kind in (0, 1):
            for way in range(2):
                rs_copy(h, way, kind, q).start()

    def sums(h, q, step):
        ring, part, kinds = ((ring0, 'first', (0,)), (ring1, 'all', (1, 2)), (ring2, 'all', (3,)))[step - 1]
        for way in range(2):
            for kind in kinds:
                rs_copy(h, way, kind, q).wait_recv()
            lo, size = rows_of(way, step, part)
            acc[h, q, lo:lo + size, :] = acc[h, q, lo:lo + size, :] + ring[h, way, q]
            rs_copy(h, way, step + 1, q).start()

    def finish(h, q):
        for way in range(2):
            rs_copy(h, way, 4, q).wait_recv()
        out_ref[h * hr:(h + 1) * hr, q * COLS:(q + 1) * COLS] = (
            acc[h, q, 0:hr, :] + (ring3[h, 0, q] + ring3[h, 1, q])).astype(out_ref.dtype)

    def experts(h, between):
        for e in range(n_exp):
            if h == 0:
                for copy in gate_copies(e):
                    copy.wait()
            for n in range(ffn // 512):
                gate_up(e, n)
                between(e * (ffn // 512) + n)

    def results(h, between):
        if h == 0:
            down_copy(0).wait()
        project(h, 0)
        for q in range(n_col):
            if h == 0 and q + 1 < n_col:
                down_copy(q + 1).wait()
            if q >= 2:
                sum_copy(h, q - 2).wait_send()
            elif h > 0:
                sum_copy(h - 1, n_col - 2 + q).wait_send()
            die_out[q % 2] = added(h, q, 1)
            acc[h, q] = added(h, q, 0)
            if q + 1 < n_col:
                project(h, q + 1)
            sum_copy(h, q).start()
            between(q)

    a, b = 0, 1
    for way in range(2):
        ring_meta(way, 1).start()
    die_meta(0).start()
    for p in range(PIECES):
        send_own_block(a, p)
    send_own_block(b, 0)
    take_meta(1)
    take_blocks(a, 1)
    send_own_block(b, 1)
    take_meta(2)
    take_blocks(a, 2)
    take_block(b, 1, 0)
    take_meta(3)
    take_blocks(a, 3)
    take_block(b, 1, 1)
    take_meta(4)
    for j in range(nz):
        die_meta(j).wait_recv()
    for h in range(HALVES):
        for other in range(CORES):
            one_hots(h, other, h == a, True)
    take_blocks(a, 4)
    take_block(b, 2, 0)
    die_ready(a)
    gather(a)
    for other in range(CORES):
        one_hots(b, other, True, False)
    take_block(b, 2, 1)

    def after_a(k):
        if k == 0:
            take_block(b, 3, 0)
        if k == 2:
            take_block(b, 3, 1)
        if k == 5:
            take_blocks(b, 4)

    experts(a, after_a)

    def after_ra(q):
        if q >= 1:
            own_sums(a, q - 1)

    results(a, after_ra)
    sums(a, 0, 1)
    die_ready(b)
    gather(b)

    plan = {0: [('own', 3), (1, 1)], 1: [(2, 0)], 2: [(1, 2)], 3: [(2, 1)], 4: [(1, 3), (3, 0)], 5: [(2, 2)],
            6: [(3, 1)], 7: [(2, 3)]}

    def after_b(k):
        for step, q in plan.get(k, ()):
            if step == 'own':
                own_sums(a, q)
            else:
                sums(a, q, step)

    experts(b, after_b)

    def after_rb(q):
        if q == 0:
            sums(a, 2, 3)
            finish(a, 0)
        if q == 1:
            own_sums(b, 0)
            sums(a, 3, 3)
            finish(a, 1)
        if q == 2:
            own_sums(b, 1)
            finish(a, 2)
        if q == 3:
            own_sums(b, 2)
            finish(a, 3)

    results(b, after_rb)
    sums(b, 0, 1)
    own_sums(b, 3)
    for q in range(1, n_col):
        sums(b, q, 1)
    for step in (2, 3):
        for q in range(n_col):
            sums(b, q, step)
    for q in range(n_col):
        finish(b, q)

    for way in range(2):
        for hop in range(1, far + 1):
            if meta_on_ring(way, hop):
                ring_meta(way, hop).wait_send()
            for p in range(PIECES):
                if on_ring(way, hop, p):
                    for h in range(HALVES):
                        ring_copy(h, way, hop, p).wait_send()
    for j in range(nz):
        die_meta(j).wait_send()
        for p in range(PIECES):
            for h in range(HALVES):
                die_copy(h, j, p).wait_send()
    for q in range(n_col - 2, n_col):
        sum_copy(b, q).wait_send()
    for h in range(HALVES):
        for way in range(2):
            for kind in range(5):
                for q in range(n_col):
                    rs_copy(h, way, kind, q).wait_send()


def solution(mesh):
    row_spec = P(('dp', 'ep'), None)
    exp_spec = P('ep', None, None)
    devs = mesh.shape['ep']
    nz = devs // CORES

    def local_moe(tok_rows, expert_ids, gate_weights, slot_ids, w_gate, w_up, w_down):
        rows, dim = tok_rows.shape
        top_k = expert_ids.shape[1]
        n_exp, _, ffn = w_gate.shape
        capacity = 2 * top_k * rows // n_exp
        n_col = dim // COLS
        far = nz // 2
        hr = rows // HALVES
        slots = n_exp * capacity
        half_tok = devs * hr
        dma = pltpu.SemaphoreType.DMA
        vmem = pltpu.VMEM
        scratch = [
            vmem((top_k, rows), jnp.int32), vmem((top_k, rows), jnp.int32), vmem((top_k, rows), F32),
            vmem((HALVES, devs, hr, dim), BF16), vmem((devs, 8, 128), F32),
            vmem((n_exp, dim, ffn), BF16), vmem((n_exp, dim, ffn), BF16), vmem((n_col, n_exp, ffn, COLS), BF16),
            vmem((slots, half_tok), BF16), vmem((HALVES, half_tok, slots), BF16), vmem((slots, 128), F32),
            vmem((slots, dim), BF16), vmem((slots, ffn), BF16), vmem((3, slots, COLS), BF16), vmem((3, slots, COLS), BF16),
            vmem((HALVES, n_col, nz * hr, COLS), F32), vmem((2, nz * hr, COLS), F32), vmem((HALVES, n_col, nz * hr, COLS), F32),
            vmem((HALVES, 2, n_col, hr // 2, COLS), F32), vmem((HALVES, 2, n_col, hr, COLS), F32),
            vmem((HALVES, 2, n_col, hr, COLS), F32), vmem((HALVES, 2, n_col, hr, COLS), F32),
            dma((HALVES,)), dma((3,)), dma((n_exp, 2)), dma((n_col,)),
            dma((HALVES, 2, far, PIECES)), dma((HALVES, 2, far, PIECES)), dma((2, far)), dma((2, far)),
            dma((HALVES, nz, PIECES)), dma((HALVES, nz, PIECES)), dma((nz,)), dma((nz,)),
            dma((HALVES, n_col)), dma((HALVES, n_col)),
            dma((HALVES, 2, 5, n_col)), dma((HALVES, 2, 5, n_col)),
        ]
        anyspace = pl.BlockSpec(memory_space=pl.ANY)
        flops = 6 * slots * dim * ffn
        return pl.pallas_call(
            functools.partial(moe_kernel, nz, capacity),
            out_shape=jax.ShapeDtypeStruct((rows, dim), tok_rows.dtype),
            in_specs=[anyspace] * 7,
            out_specs=pl.BlockSpec(memory_space=pltpu.VMEM),
            scratch_shapes=scratch,
            name='routed_experts',
            cost_estimate=pl.CostEstimate(flops=flops, bytes_accessed=6 * n_exp * dim * ffn, transcendentals=slots * ffn),
            compiler_params=pltpu.CompilerParams(
                collective_id=0, has_side_effects=True, vmem_limit_bytes=67043328),
        )(tok_rows, expert_ids.T, slot_ids.T, gate_weights.T, w_gate, w_up, w_down)

    return jax.shard_map(local_moe, mesh=mesh, in_specs=(row_spec, row_spec, row_spec, row_spec, exp_spec, exp_spec, exp_spec), out_specs=row_spec, check_vma=False)
```

time: 208 us -> 72.8 us (0.35)
  the two profiles are of different devices: /device:TPU:21 before, /device:TPU:22 now
where the time goes in v3:
time: 72.8 us; the launch traced here: 72.7 us
  Pallas kernels  71.1 us (98%)
  local copies, waits for them, and re-layouts  1.57 us (2%)
    pallas_call x1, Pallas kernels, local_moe(): pl.pallas_call(functools.partial(moe_kernel, nz, capacity), out_shape=jax...  71.1 us
    unnamed x1, local copies, waits for them, and re-layouts  1.57 us

profile of v3, /device:TPU:22, one launch (start us, length us, event | category | flops | bytes accessed | tf_op | source)
XLA Modules:
  0.0 72.7 jit_solution(17601624370323037792)
XLA Ops:
  0.0 71.1 %routed_experts.1 = bf16[32,2048]{1,0:T(8,128)(2,1)} custom-call(bf16[32,2048]{1,0:T(8,128)(2,1)} %tok_hbm.1, s32[8,32]{1,0:T(8,128)} %bitcast.3, s32[8,32]{1,0:T(8,128)} %bitcast.4, f32[8,32]{1,0:T(8,128)} %bitcast.5, bf16[4,2048,1024]{2,1,0:T(8,128)(2,1)} %wg_hbm.1, bf16[4,2048,1024]{2,1,0:T(8,128)(2,1)} %wu_hbm.1, bf16[4,1024,2048]{2,1,0:T(8,128)(2,1)} %wd_hbm.1), custom_call_target="tpu_custom_call" | custom-call | flops 6442450944 | bytes 50331648 | tf_op jit(solution)/shard_map/routed_experts/pallas_call | solution.py:427
  71.1 1.6 %copy.9 = bf16[32,2048]{1,0:T(8,128)(2,1)} copy(bf16[32,2048]{1,0:T(8,128)(2,1)} %routed_experts.1) | data formatting | bytes 262144

commit v4 on v2

--- a/solution.py
+++ b/solution.py
@@ -9,8 +9,9 @@
 
 CORES = 2
 PIECES = 4
-COLS = 256
-DOWN_SLOTS = 6
+COLS = 512
+DOWN_SLOTS = 3
+LAGS = (3, 99)
 MESH = pl.DeviceIdType.MESH
 F32 = jnp.float32
 BF16 = jnp.bfloat16
@@ -48,8 +49,8 @@
         copy.start()
 
     def gate_copies(e):
-        return (pltpu.make_async_copy(wg_hbm.at[e], wg.at[e], gate_sem.at[e, 0]),
-                pltpu.make_async_copy(wu_hbm.at[e], wu.at[e], gate_sem.at[e, 1]))
+        return (pltpu.make_async_copy(wg_hbm.at[e], wg.at[e], gate_sem.at[0]),
+                pltpu.make_async_copy(wu_hbm.at[e], wu.at[e], gate_sem.at[1]))
 
     def down_copy(q):
         cols = pl.ds(pl.multiple_of(q * COLS, COLS), COLS)
@@ -79,6 +80,9 @@
     def spot(other, j):
         return (place[j] // quad) * nz + other * quad + place[j] % quad
 
+    def landed(ref, sem):
+        pltpu.make_async_copy(ref, ref, sem).wait()
+
     def cols_of(p):
         return pl.ds(p * piece, piece)
 
@@ -87,23 +91,23 @@
         dst = nz - hop if way == 0 else hop
         return pltpu.make_async_remote_copy(
             tok_all.at[spot(0, src), :, cols_of(p)], tok_all.at[spot(0, dst), :, cols_of(p)],
-            ag_send.at[way, hop - 1, p], ag_recv.at[way, hop - 1, p], device_id=nbr[way], device_id_type=MESH)
+            ag_send, ag_recv.at[way, hop - 1, p], device_id=nbr[way], device_id_type=MESH)
 
     def ring_meta(way, hop):
         src = (nz - hop + 1) % nz if way == 0 else hop - 1
         dst = nz - hop if way == 0 else hop
         return pltpu.make_async_remote_copy(
-            meta_all.at[spot(0, src)], meta_all.at[spot(0, dst)], agm_send.at[way, hop - 1], agm_recv.at[way, hop - 1],
+            meta_all.at[spot(0, src)], meta_all.at[spot(0, dst)], agm_send, agm_recv.at[way, hop - 1],
             device_id=nbr[way], device_id_type=MESH)
 
     def die_copy(j, p):
         return pltpu.make_async_remote_copy(
             tok_all.at[spot(0, j), :, cols_of(p)], tok_all.at[spot(1, j), :, cols_of(p)],
-            die_send.at[j, p], die_recv.at[j, p], device_id=partner, device_id_type=MESH)
+            die_send, die_recv.at[place[j] // quad], device_id=partner, device_id_type=MESH)
 
     def die_meta(j):
         return pltpu.make_async_remote_copy(
-            meta_all.at[spot(0, j)], meta_all.at[spot(1, j)], diem_send.at[j], diem_recv.at[j],
+            meta_all.at[spot(0, j)], meta_all.at[spot(1, j)], diem_send, diem_recv.at[place[j] // quad],
             device_id=partner, device_id_type=MESH)
 
     def on_ring(way, hop, p):
@@ -132,8 +136,10 @@
                     ring_meta(way, hop + 1).start()
                 die_meta(nz - hop if way == 0 else hop).start()
 
-    def take_tokens(hop):
-        for p in range(PIECES):
+    def take_tokens(hop, pieces=range(PIECES), fill=()):
+        for p in pieces:
+            for work in fill[p:p + 1]:
+                work()
             for way in range(2):
                 if on_ring(way, hop, p):
                     ring_copy(way, hop, p).wait_recv()
@@ -173,10 +179,9 @@
             pick_t[base:base + 128, e * capacity:(e + 1) * capacity] = jnp.where(
                 slot_lane == table[:, e:e + 1], 1.0, 0.0).astype(BF16)
 
-    def gather(part):
-        @pl.loop(0, dim // 512)
-        def _(n):
-            cols = pl.ds(pl.multiple_of(n * 512, 512), 512)
+    def gather(part, blocks):
+        for n in blocks:
+            cols = slice(n * 512, (n + 1) * 512)
             block = tok_all[part * nz:(part + 1) * nz, :, cols].reshape(nz * rows, 512)
             got = jnp.dot(pick[:, part * nz * rows:(part + 1) * nz * rows], block, preferred_element_type=F32)
             if part == 0:
@@ -184,34 +189,35 @@
             else:
                 buf[:, cols] = (buf[:, cols].astype(F32) + got).astype(BF16)
 
-    def die_ready(blocks):
-        for j in blocks:
-            for p in range(PIECES):
-                die_copy(j, p).wait_recv()
-
+    def others(part):
+        return slice(part * nz + quad, (part + 1) * nz)
+
+    def near_routes():
+        landed(meta_all.at[others(0)], diem_recv.at[0])
+
+    def near_blocks():
+        landed(tok_all.at[others(0)], die_recv.at[0])
+        gather(0, (0,))
+
+    wide = range(dim // 512)
+    fills = {2: [lambda: None, near_routes, lambda: one_hots(0), lambda: one_hots(1)],
+             3: [lambda: None, near_blocks] + [functools.partial(gather, 0, (n,)) for n in wide[1:3]]}
     for hop in range(1, far):
         take_meta(hop)
-        take_tokens(hop)
-    for j in order[:quad]:
-        die_meta(j).wait_recv()
-    one_hots(0)
-    one_hots(1)
-    die_ready(order[:quad])
-    gather(0)
+        take_tokens(hop, fill=fills.get(hop, ()))
     take_meta(far)
-    for j in order[quad:]:
-        die_meta(j).wait_recv()
+    gather(0, wide[3:])
+    take_tokens(far, range(0, PIECES, 2))
+    landed(meta_all.at[others(1)], diem_recv.at[1])
     one_hots(2)
+    take_tokens(far, range(1, PIECES, 2))
     one_hots(3)
-    take_tokens(far)
-    die_ready(order[quad:])
-    gather(1)
-
-    @pl.loop(0, n_exp)
-    def _(e):
-        for copy in gate_copies(e):
-            copy.wait()
-        here = pl.ds(pl.multiple_of(e * capacity, capacity), capacity)
+    landed(tok_all.at[others(1)], die_recv.at[1])
+    landed(wg, gate_sem.at[0])
+    landed(wu, gate_sem.at[1])
+    gather(1, wide)
+    for e in range(n_exp):
+        here = slice(e * capacity, (e + 1) * capacity)
         for n in range(ffn // 512):
             cols = slice(n * 512, (n + 1) * 512)
             x = buf[here, :]
@@ -239,7 +245,7 @@
         else:
             to = dst.at[way, q, pl.ds(part.start, part.stop - part.start), :]
         return pltpu.make_async_remote_copy(
-            src, to, rs_send.at[way, kind, q], rs_recv.at[way, kind, q], device_id=nbr[way], device_id_type=MESH)
+            src, to, rs_send.at[step], rs_recv.at[step, q], device_id=nbr[way], device_id_type=MESH)
 
     def send_own(q):
         sum_copy(q).wait_recv()
@@ -248,6 +254,19 @@
             for way in range(2):
                 rs_copy(way, kind, q).start()
 
+    rings = (ring0, ring1, ring2, ring3)
+
+    def sums(q, step):
+        landed(rings[step - 1].at[:, q], rs_recv.at[step - 1, q])
+        for way in range(2):
+            lo = place[block_of(way, step)] * rows
+            size = rows
+            if step == 1:
+                lo, size = lo + (0 if way == 0 else half), half
+            acc[q, lo:lo + size, :] = acc[q, lo:lo + size, :] + rings[step - 1][way, q]
+            rs_copy(way, step + 1, q).start()
+
+    done = {1: 0, 2: 0, 3: 0}
     parts = (parts_a, parts_b)
 
     def project(q):
@@ -286,53 +305,28 @@
             down_copy(q + DOWN_SLOTS).start(priority=1)
         if q >= 1:
             send_own(q - 1)
+        for step in (1, 2):
+            if q >= LAGS[step - 1]:
+                sums(q - LAGS[step - 1], step)
+                done[step] = q - LAGS[step - 1] + 1
 
     send_own(n_col - 1)
-
-    @pl.loop(0, n_col)
-    def _(q):
-        for way in range(2):
-            rs_copy(way, 0, q).wait_recv()
-            lo = place[block_of(way, 1)] * rows + (0 if way == 0 else half)
-            acc[q, lo:lo + half, :] = acc[q, lo:lo + half, :] + ring0[way, q]
-            rs_copy(way, 2, q).start()
-
-    for step, ring, kinds in ((2, ring1, (1, 2)), (3, ring2, (3,))):
-        @pl.loop(0, n_col)
-        def _(q):
-            for way in range(2):
-                for kind in kinds:
-                    rs_copy(way, kind, q).wait_recv()
-                lo = place[block_of(way, step)] * rows
-                acc[q, lo:lo + rows, :] = acc[q, lo:lo + rows, :] + ring[way, q]
-                rs_copy(way, step + 1, q).start()
-
-    @pl.loop(0, n_col)
-    def _(q):
-        for way in range(2):
-            rs_copy(way, 4, q).wait_recv()
-        cols = pl.ds(pl.multiple_of(q * COLS, COLS), COLS)
+    for step in (1, 2, 3):
+        for q in range(done[step], n_col):
+            sums(q, step)
+    for q in range(n_col):
+        landed(ring3.at[:, q], rs_recv.at[3, q])
+        cols = slice(q * COLS, (q + 1) * COLS)
         out_ref[:, cols] = (acc[q, 0:rows, :] + (ring3[0, q] + ring3[1, q])).astype(out_ref.dtype)
 
-    for way in range(2):
-        for hop in range(1, far + 1):
-            if meta_on_ring(way, hop):
-                ring_meta(way, hop).wait_send()
-            for p in range(PIECES):
-                if on_ring(way, hop, p):
-                    ring_copy(way, hop, p).wait_send()
-    for j in range(nz):
-        die_meta(j).wait_send()
-        for p in range(PIECES):
-            die_copy(j, p).wait_send()
+    landed(tok_all.at[0:nz - 1], ag_send)
+    landed(tok_all.at[0:nz], die_send)
+    landed(meta_all.at[0:nz - 1], agm_send)
+    landed(meta_all.at[0:nz], diem_send)
     for q in range(max(n_col - 2, 0), n_col):
         sum_copy(q).wait_send()
-
-    @pl.loop(0, n_col)
-    def _(q):
-        for way in range(2):
-            for kind in range(5):
-                rs_copy(way, kind, q).wait_send()
+    for ring in range(4):
+        landed(rings[ring], rs_send.at[ring])
 
 
 def solution(mesh):
@@ -362,11 +356,10 @@
             vmem((n_col, nz * rows, COLS), F32), vmem((2, nz * rows, COLS), F32), vmem((n_col, nz * rows, COLS), F32),
             vmem((2, n_col, rows // 2, COLS), F32),
             vmem((2, n_col, rows, COLS), F32), vmem((2, n_col, rows, COLS), F32), vmem((2, n_col, rows, COLS), F32),
-            dma, dma((3,)), dma((n_exp, 2)), dma((n_col,)),
-            dma((2, far, PIECES)), dma((2, far, PIECES)), dma((2, far)), dma((2, far)),
-            dma((nz, PIECES)), dma((nz, PIECES)), dma((nz,)), dma((nz,)),
-            dma((2,)), dma((n_col,)),
-            dma((2, 5, n_col)), dma((2, 5, n_col)),
+            dma, dma((3,)), dma((2,)), dma((n_col,)),
+            dma, dma((2, far, PIECES)), dma, dma((2, far)),
+            dma, dma((2,)), dma, dma((2,)),
+            dma((2,)), dma((n_col,)), dma((4,)), dma((4, n_col)),
         ]
         anyspace = pl.BlockSpec(memory_space=pl.ANY)
         in_vmem = pl.BlockSpec(memory_space=pltpu.VMEM)

time: 64.8 us -> 60.2 us (0.929)
  Pallas kernels: 63.2 us -> 58.6 us
    pallas_call x1, Pallas kernels: 63.2 us -> 58.6 us  [local_moe(): pl.pallas_call(functools.partial(moe_kernel, nz, capacity), out_shape=jax...]
where the time goes in v4:
time: 60.2 us; the launch traced here: 60.1 us
  Pallas kernels  58.6 us (97%)
  local copies, waits for them, and re-layouts  1.57 us (3%)
    pallas_call x1, Pallas kernels, local_moe(): pl.pallas_call(functools.partial(moe_kernel, nz, capacity), out_shape=jax...  58.6 us
    unnamed x1, local copies, waits for them, and re-layouts  1.57 us

profile of v4, /device:TPU:21, one launch (start us, length us, event | category | flops | bytes accessed | tf_op | source)
XLA Modules:
  0.0 60.1 jit_solution(8786068126701177933)
XLA Ops:
  0.0 58.6 %routed_experts.1 = bf16[32,2048]{1,0:T(8,128)(2,1)} custom-call(bf16[32,2048]{1,0:T(8,128)(2,1)} %tok_hbm.1, s32[8,32]{1,0:T(8,128)} %bitcast.3, s32[8,32]{1,0:T(8,128)} %bitcast.4, f32[8,32]{1,0:T(8,128)} %bitcast.5, bf16[4,2048,1024]{2,1,0:T(8,128)(2,1)} %wg_hbm.1, bf16[4,2048,1024]{2,1,0:T(8,128)(2,1)} %wu_hbm.1, bf16[4,1024,2048]{2,1,0:T(8,128)(2,1)} %wd_hbm.1), custom_call_target="tpu_custom_call" | custom-call | flops 6442450944 | bytes 50331648 | tf_op jit(solution)/shard_map/routed_experts/pallas_call | solution.py:367
  58.6 1.6 %copy.9 = bf16[32,2048]{1,0:T(8,128)(2,1)} copy(bf16[32,2048]{1,0:T(8,128)(2,1)} %routed_experts.1) | data formatting | bytes 262144

commit v5 on v4

--- a/solution.py
+++ b/solution.py
@@ -10,15 +10,13 @@
 CORES = 2
 PIECES = 4
 COLS = 512
-DOWN_SLOTS = 3
-LAGS = (3, 99)
 MESH = pl.DeviceIdType.MESH
 F32 = jnp.float32
 BF16 = jnp.bfloat16
 
 
 def moe_kernel(nz, capacity, tok_hbm, ids_hbm, slots_hbm, gates_hbm, wg_hbm, wu_hbm, wd_hbm, out_ref,
-               ids_ref, slots_ref, gates_ref, tok_all, meta_all, wg, wu, wd, pick, pick_t, slot_gate, buf, hid, parts_a, parts_b,
+               ids_ref, slots_ref, gates_ref, tok_all, meta_all, wg, wu, wd, pick, pick_t, slot_gate, buf, hid,
                acc, die_out, die_in, ring0, ring1, ring2, ring3,
                in_sem, route_sem, gate_sem, down_sem, ag_send, ag_recv, agm_send, agm_recv, die_send, die_recv,
                diem_send, diem_recv, sum_send, sum_recv, rs_send, rs_recv):
@@ -54,12 +52,12 @@
 
     def down_copy(q):
         cols = pl.ds(pl.multiple_of(q * COLS, COLS), COLS)
-        return pltpu.make_async_copy(wd_hbm.at[:, :, cols], wd.at[lax.rem(q, DOWN_SLOTS)], down_sem.at[q])
+        return pltpu.make_async_copy(wd_hbm.at[:, :, cols], wd.at[q], down_sem)
 
     for e in range(n_exp):
         for copy in gate_copies(e):
             copy.start(priority=1)
-    for q in range(min(DOWN_SLOTS, n_col)):
+    for q in range(n_col):
         down_copy(q).start(priority=1)
 
     for copy in routes:
@@ -215,6 +213,7 @@
     landed(tok_all.at[others(1)], die_recv.at[1])
     landed(wg, gate_sem.at[0])
     landed(wu, gate_sem.at[1])
+    landed(wd, down_sem)
     gather(1, wide)
     for e in range(n_exp):
         here = slice(e * capacity, (e + 1) * capacity)
@@ -225,9 +224,15 @@
             up_h = jnp.dot(x, wu[e, :, cols], preferred_element_type=F32)
             hid[here, cols] = (jax.nn.silu(gate_h) * up_h).astype(BF16)
 
-    def sum_copy(q):
-        return pltpu.make_async_remote_copy(
-            die_out.at[lax.rem(q, 2)], die_in.at[q], sum_send.at[lax.rem(q, 2)], sum_recv.at[q],
+    split = (nz - 3) * rows
+
+    def span_of(part):
+        return slice(split, side) if part == 0 else slice(0, split)
+
+    def sum_copy(q, part):
+        span = span_of(part)
+        return pltpu.make_async_remote_copy(
+            die_out.at[q, span], die_in.at[q, span], sum_send, sum_recv.at[part, q],
             device_id=partner, device_id_type=MESH)
 
     def block_of(way, step):
@@ -248,11 +253,15 @@
             src, to, rs_send.at[step], rs_recv.at[step, q], device_id=nbr[way], device_id_type=MESH)
 
     def send_own(q):
-        sum_copy(q).wait_recv()
-        acc[q] = acc[q] + die_in[q]
+        sum_copy(q, 0).wait_recv()
+        acc[q, split:side, :] = acc[q, split:side, :] + die_in[q, split:side, :]
         for kind in (0, 1):
             for way in range(2):
                 rs_copy(way, kind, q).start()
+
+    def add_rest(q):
+        sum_copy(q, 1).wait_recv()
+        acc[q, 0:split, :] = acc[q, 0:split, :] + die_in[q, 0:split, :]
 
     rings = (ring0, ring1, ring2, ring3)
 
@@ -266,67 +275,63 @@
             acc[q, lo:lo + size, :] = acc[q, lo:lo + size, :] + rings[step - 1][way, q]
             rs_copy(way, step + 1, q).start()
 
-    done = {1: 0, 2: 0, 3: 0}
-    parts = (parts_a, parts_b)
+    slots = n_exp * capacity
 
     def project(q):
-        into = parts[q % 2]
         for e in range(n_exp):
             span = slice(e * capacity, (e + 1) * capacity)
-            res = jnp.dot(hid[span, :], wd[q % DOWN_SLOTS, e], preferred_element_type=F32)
+            res = jnp.dot(hid[span, :], wd[q, e], preferred_element_type=F32)
             res = res * jnp.concatenate([slot_gate[span, :]] * (COLS // 128), axis=1)
             hi = res.astype(BF16)
             rest = res - hi.astype(F32)
             mid = rest.astype(BF16)
-            into[0, span, :] = hi
-            into[1, span, :] = mid
-            into[2, span, :] = (rest - mid.astype(F32)).astype(BF16)
-
-    def added(q, lo):
-        onehot = pick_t[lo:lo + side, :]
-        part = parts[q % 2]
-        return (jnp.dot(onehot, part[0], preferred_element_type=F32)
-                + jnp.dot(onehot, part[1], preferred_element_type=F32)
-                + jnp.dot(onehot, part[2], preferred_element_type=F32))
-
-    down_copy(0).wait()
+            low = (rest - mid.astype(F32)).astype(BF16)
+            for i, value in enumerate((hi, mid, low)):
+                wg[q, i * slots + e * capacity:i * slots + (e + 1) * capacity, 0:COLS] = value
+
+    def add_up(q, part):
+        span = span_of(part)
+        size = span.stop - span.start
+        onehot = jnp.concatenate(
+            [pick_t[span, :], pick_t[side + span.start:side + span.stop, :]], axis=0)
+        total = jnp.dot(onehot, wg[q, 0:slots, 0:COLS], preferred_element_type=F32)
+        for i in (1, 2):
+            total = total + jnp.dot(onehot, wg[q, i * slots:(i + 1) * slots, 0:COLS], preferred_element_type=F32)
+        acc[q, span, :] = total[0:size]
+        die_out[q, span, :] = total[size:2 * size]
+
     project(0)
     for q in range(n_col):
-        if q + 1 < n_col:
-            down_copy(q + 1).wait()
-        if q >= 2:
-            sum_copy(q - 2).wait_send()
-        die_out[q % 2] = added(q, side)
-        acc[q] = added(q, 0)
+        add_up(q, 0)
         if q + 1 < n_col:
             project(q + 1)
-        sum_copy(q).start()
-        if q + DOWN_SLOTS < n_col:
-            down_copy(q + DOWN_SLOTS).start(priority=1)
+        sum_copy(q, 0).start()
         if q >= 1:
             send_own(q - 1)
-        for step in (1, 2):
-            if q >= LAGS[step - 1]:
-                sums(q - LAGS[step - 1], step)
-                done[step] = q - LAGS[step - 1] + 1
-
-    send_own(n_col - 1)
-    for step in (1, 2, 3):
-        for q in range(done[step], n_col):
+    for q in range(n_col):
+        add_up(q, 1)
+        sum_copy(q, 1).start()
+        if q == 0:
+            send_own(n_col - 1)
+        sums(q, 1)
+    for step in (2, 3):
+        for q in range(n_col):
+            if step == 2:
+                add_rest(q)
             sums(q, step)
+    landed(tok_all.at[0:nz - 1], ag_send)
+    landed(tok_all.at[0:nz], die_send)
+    landed(meta_all.at[0:nz - 1], agm_send)
+    landed(meta_all.at[0:nz], diem_send)
+    landed(die_out, sum_send)
+    for ring in range(3):
+        landed(rings[ring], rs_send.at[ring])
     for q in range(n_col):
         landed(ring3.at[:, q], rs_recv.at[3, q])
         cols = slice(q * COLS, (q + 1) * COLS)
         out_ref[:, cols] = (acc[q, 0:rows, :] + (ring3[0, q] + ring3[1, q])).astype(out_ref.dtype)
 
-    landed(tok_all.at[0:nz - 1], ag_send)
-    landed(tok_all.at[0:nz], die_send)
-    landed(meta_all.at[0:nz - 1], agm_send)
-    landed(meta_all.at[0:nz], diem_send)
-    for q in range(max(n_col - 2, 0), n_col):
-        sum_copy(q).wait_send()
-    for ring in range(4):
-        landed(rings[ring], rs_send.at[ring])
+    landed(ring3, rs_send.at[3])
 
 
 def solution(mesh):
@@ -350,16 +355,16 @@
             vmem((top_k, rows), jnp.int32), vmem((top_k, rows), jnp.int32), vmem((top_k, rows), F32),
             vmem((devs, rows, dim), BF16), vmem((devs, 8, 128), F32),
             vmem((n_exp, dim, ffn), BF16), vmem((n_exp, dim, ffn), BF16),
-            vmem((min(DOWN_SLOTS, n_col), n_exp, ffn, COLS), BF16),
+            vmem((n_col, n_exp, ffn, COLS), BF16),
             vmem((slots, total), BF16), vmem((total, slots), BF16), vmem((slots, 128), F32),
-            vmem((slots, dim), BF16), vmem((slots, ffn), BF16), vmem((3, slots, COLS), BF16), vmem((3, slots, COLS), BF16),
-            vmem((n_col, nz * rows, COLS), F32), vmem((2, nz * rows, COLS), F32), vmem((n_col, nz * rows, COLS), F32),
+            vmem((slots, dim), BF16), vmem((slots, ffn), BF16),
+            vmem((n_col, nz * rows, COLS), F32), vmem((n_col, nz * rows, COLS), F32), vmem((n_col, nz * rows, COLS), F32),
             vmem((2, n_col, rows // 2, COLS), F32),
             vmem((2, n_col, rows, COLS), F32), vmem((2, n_col, rows, COLS), F32), vmem((2, n_col, rows, COLS), F32),
-            dma, dma((3,)), dma((2,)), dma((n_col,)),
+            dma, dma((3,)), dma((2,)), dma,
             dma, dma((2, far, PIECES)), dma, dma((2, far)),
             dma, dma((2,)), dma, dma((2,)),
-            dma((2,)), dma((n_col,)), dma((4,)), dma((4, n_col)),
+            dma, dma((2, n_col)), dma((4,)), dma((4, n_col)),
         ]
         anyspace = pl.BlockSpec(memory_space=pl.ANY)
         in_vmem = pl.BlockSpec(memory_space=pltpu.VMEM)

time: 60.2 us -> 58.1 us (0.965)
  Pallas kernels: 58.6 us -> 56.4 us
    pallas_call x1, Pallas kernels: 58.6 us -> 56.4 us  [local_moe(): pl.pallas_call(functools.partial(moe_kernel, nz, capacity), out_shape=jax...]
where the time goes in v5:
time: 58.1 us; the launch traced here: 58 us
  Pallas kernels  56.4 us (97%)
  local copies, waits for them, and re-layouts  1.57 us (3%)
    pallas_call x1, Pallas kernels, local_moe(): pl.pallas_call(functools.partial(moe_kernel, nz, capacity), out_shape=jax...  56.4 us
    unnamed x1, local copies, waits for them, and re-layouts  1.57 us

profile of v5, /device:TPU:21, one launch (start us, length us, event | category | flops | bytes accessed | tf_op | source)
XLA Modules:
  0.0 58.0 jit_solution(11675401918096114594)
XLA Ops:
  0.0 56.4 %routed_experts.1 = bf16[32,2048]{1,0:T(8,128)(2,1)} custom-call(bf16[32,2048]{1,0:T(8,128)(2,1)} %tok_hbm.1, s32[8,32]{1,0:T(8,128)} %bitcast.3, s32[8,32]{1,0:T(8,128)} %bitcast.4, f32[8,32]{1,0:T(8,128)} %bitcast.5, bf16[4,2048,1024]{2,1,0:T(8,128)(2,1)} %wg_hbm.1, bf16[4,2048,1024]{2,1,0:T(8,128)(2,1)} %wu_hbm.1, bf16[4,1024,2048]{2,1,0:T(8,128)(2,1)} %wd_hbm.1), custom_call_target="tpu_custom_call" | custom-call | flops 6442450944 | bytes 50331648 | tf_op jit(solution)/shard_map/routed_experts/pallas_call | solution.py:372
  56.4 1.6 %copy.9 = bf16[32,2048]{1,0:T(8,128)(2,1)} copy(bf16[32,2048]{1,0:T(8,128)(2,1)} %routed_experts.1) | data formatting | bytes 262144

commit v6 on v5

--- a/solution.py
+++ b/solution.py
@@ -116,12 +116,12 @@
     def meta_on_ring(way, hop):
         return hop < far or (hop == far and way == 0)
 
-    for way in range(2):
-        ring_meta(way, 1).start()
     for p in range(PIECES):
         for way in range(2):
             if on_ring(way, 1, p):
                 ring_copy(way, 1, p).start()
+            if p == 0:
+                ring_meta(way, 1).start()
     die_meta(0).start()
     for p in range(PIECES):
         die_copy(0, p).start()
@@ -204,12 +204,12 @@
         take_meta(hop)
         take_tokens(hop, fill=fills.get(hop, ()))
     take_meta(far)
-    gather(0, wide[3:])
     take_tokens(far, range(0, PIECES, 2))
+    take_tokens(far, range(1, PIECES, 2))
     landed(meta_all.at[others(1)], diem_recv.at[1])
     one_hots(2)
-    take_tokens(far, range(1, PIECES, 2))
     one_hots(3)
+    gather(0, wide[3:])
     landed(tok_all.at[others(1)], die_recv.at[1])
     landed(wg, gate_sem.at[0])
     landed(wu, gate_sem.at[1])
@@ -313,12 +313,14 @@
         sum_copy(q, 1).start()
         if q == 0:
             send_own(n_col - 1)
+        else:
+            add_rest(q - 1)
         sums(q, 1)
     for step in (2, 3):
         for q in range(n_col):
-            if step == 2:
-                add_rest(q)
             sums(q, step)
+            if step == 2 and q == 0:
+                add_rest(n_col - 1)
     landed(tok_all.at[0:nz - 1], ag_send)
     landed(tok_all.at[0:nz], die_send)
     landed(meta_all.at[0:nz - 1], agm_send)

time: 58.1 us -> 58.5 us (level)
  no operation moved by 1% of the time
where the time goes in v6:
time: 58.5 us; the launch traced here: 58.4 us
  Pallas kernels  56.8 us (97%)
  local copies, waits for them, and re-layouts  1.57 us (3%)
    pallas_call x1, Pallas kernels, local_moe(): pl.pallas_call(functools.partial(moe_kernel, nz, capacity), out_shape=jax...  56.8 us
    unnamed x1, local copies, waits for them, and re-layouts  1.57 us

profile of v6, /device:TPU:21, one launch (start us, length us, event | category | flops | bytes accessed | tf_op | source)
XLA Modules:
  0.0 58.4 jit_solution(12247256761661887806)
XLA Ops:
  0.0 56.8 %routed_experts.1 = bf16[32,2048]{1,0:T(8,128)(2,1)} custom-call(bf16[32,2048]{1,0:T(8,128)(2,1)} %tok_hbm.1, s32[8,32]{1,0:T(8,128)} %bitcast.3, s32[8,32]{1,0:T(8,128)} %bitcast.4, f32[8,32]{1,0:T(8,128)} %bitcast.5, bf16[4,2048,1024]{2,1,0:T(8,128)(2,1)} %wg_hbm.1, bf16[4,2048,1024]{2,1,0:T(8,128)(2,1)} %wu_hbm.1, bf16[4,1024,2048]{2,1,0:T(8,128)(2,1)} %wd_hbm.1), custom_call_target="tpu_custom_call" | custom-call | flops 6442450944 | bytes 50331648 | tf_op jit(solution)/shard_map/routed_experts/pallas_call | solution.py:374
  56.9 1.6 %copy.9 = bf16[32,2048]{1,0:T(8,128)(2,1)} copy(bf16[32,2048]{1,0:T(8,128)(2,1)} %routed_experts.1) | data formatting | bytes 262144

commit v7 on v5

--- a/solution.py
+++ b/solution.py
@@ -204,12 +204,12 @@
         take_meta(hop)
         take_tokens(hop, fill=fills.get(hop, ()))
     take_meta(far)
-    gather(0, wide[3:])
     take_tokens(far, range(0, PIECES, 2))
+    take_tokens(far, range(1, PIECES, 2))
     landed(meta_all.at[others(1)], diem_recv.at[1])
     one_hots(2)
-    take_tokens(far, range(1, PIECES, 2))
     one_hots(3)
+    gather(0, wide[3:])
     landed(tok_all.at[others(1)], die_recv.at[1])
     landed(wg, gate_sem.at[0])
     landed(wu, gate_sem.at[1])

time: 58.1 us -> 58 us (level)
  no operation moved by 1% of the time
where the time goes in v7:
time: 58 us; the launch traced here: 57.9 us
  Pallas kernels  56.3 us (97%)
  local copies, waits for them, and re-layouts  1.57 us (3%)
    pallas_call x1, Pallas kernels, local_moe(): pl.pallas_call(functools.partial(moe_kernel, nz, capacity), out_shape=jax...  56.3 us
    unnamed x1, local copies, waits for them, and re-layouts  1.57 us

profile of v7, /device:TPU:21, one launch (start us, length us, event | category | flops | bytes accessed | tf_op | source)
XLA Modules:
  0.0 57.9 jit_solution(4156276556448380953)
XLA Ops:
  0.0 56.3 %routed_experts.1 = bf16[32,2048]{1,0:T(8,128)(2,1)} custom-call(bf16[32,2048]{1,0:T(8,128)(2,1)} %tok_hbm.1, s32[8,32]{1,0:T(8,128)} %bitcast.3, s32[8,32]{1,0:T(8,128)} %bitcast.4, f32[8,32]{1,0:T(8,128)} %bitcast.5, bf16[4,2048,1024]{2,1,0:T(8,128)(2,1)} %wg_hbm.1, bf16[4,2048,1024]{2,1,0:T(8,128)(2,1)} %wu_hbm.1, bf16[4,1024,2048]{2,1,0:T(8,128)(2,1)} %wd_hbm.1), custom_call_target="tpu_custom_call" | custom-call | flops 6442450944 | bytes 50331648 | tf_op jit(solution)/shard_map/routed_experts/pallas_call | solution.py:372
  56.3 1.6 %copy.9 = bf16[32,2048]{1,0:T(8,128)(2,1)} copy(bf16[32,2048]{1,0:T(8,128)(2,1)} %routed_experts.1) | data formatting | bytes 262144
